TPU v7x, 32 devices: a whole 2x2x4 slice. The times are simulated.
32 devices in a mesh: cand: 4 (over y, core), tensor: 8 (over z, x).
Axes of the slice: x: 2, y: 2, z: 4, core: 2. Of those that a mesh axis runs over, the one named last changes fastest.
Arguments:
- states: bfloat16 [512, 3584], P('cand'), may hold values from -60 to 60
- targets: int32 [512], replicated, may hold values from 0 to 131071
- loss_mask: int32 [512], P('cand'), may hold values 0 or 1
- cand_of: int32 [4], replicated, may hold values from 0 to 3
- lambdas: float32 [4], replicated, may hold values from 0.2 to 1
- base_q: bfloat16 [3584, 4096], P('cand', 'tensor'), may hold values from -0.09375 to 0.09375
- delta_q: bfloat16 [2, 3584, 4096], P(None, 'cand', 'tensor'), may hold values from -0.046875 to 0.046875
- base_k: bfloat16 [3584, 2048], P('cand'), may hold values from -0.09375 to 0.09375
- delta_k: bfloat16 [2, 3584, 2048], P(None, 'cand'), may hold values from -0.046875 to 0.046875
- base_v: bfloat16 [3584, 2048], P('cand'), may hold values from -0.09375 to 0.09375
- delta_v: bfloat16 [2, 3584, 2048], P(None, 'cand'), may hold values from -0.046875 to 0.046875
- base_o: bfloat16 [4096, 3584], P('tensor', 'cand'), may hold values from -0.09375 to 0.09375
- delta_o: bfloat16 [2, 4096, 3584], P(None, 'tensor', 'cand'), may hold values from -0.046875 to 0.046875
- pre_gain: float32 [3584], replicated, may hold values from 0.5 to 2
- post_gain: float32 [3584], replicated, may hold values from 0.5 to 2
- final_gain: float32 [3584], replicated, may hold values from 0.5 to 2
- unembed: bfloat16 [3584, 131072], P(None, ('cand', 'tensor')), may hold values from -0.3125 to 0.3125
Outputs:
- token_loss: float32 [512], P('cand')
- cand_loss: float32 [4], replicated
All inputs are finite; a program needn't handle non-finite values. No bound on the sum of `loss_mask` on one device may be relied on, other than what follows from the above.
Results may differ from a plain program's by a relative error of at most 0.002.
Values may be sent and summed in bfloat16 or wider, within the bound.
No kernel may reach another device: no remote copies, remote signals or barrier semaphores. Data moves between devices by JAX's collectives and lax.ppermute only.
A program may use at most 128 MiB of HBM per device.

v0:
```python
import math

import jax
import jax.numpy as jnp
from jax import lax
from jax.sharding import PartitionSpec as P

KV = 8
HEAD_SIZE = 256
CANDS = 4


def root_norm(entries, scale_gain):
    mean_square = jnp.mean(entries * entries, axis=-1, keepdims=True)
    return entries * lax.rsqrt(mean_square + 1e-06) * scale_gain


def rotate_pairs(entries, length):
    half_width = entries.shape[-1] // 2
    positions = jnp.arange(length).astype(jnp.float32)
    frequency = jnp.exp(
        -math.log(10000.0) * jnp.arange(half_width).astype(jnp.float32) * 2.0 / entries.shape[-1]
    )
    angles = positions[:, None] * frequency[None, :]
    cosine = jnp.cos(angles)[:, None, :]
    sine_part = jnp.sin(angles)[:, None, :]
    first = entries[..., :half_width]
    second = entries[..., half_width:]
    return jnp.concatenate(
        [first * cosine - second * sine_part, second * cosine + first * sine_part], axis=-1
    )


def task_total(delta):
    return jnp.sum(delta.astype(jnp.float32), axis=0).astype(jnp.bfloat16)


def merge_weights(base, total, mixing):
    return (base.astype(jnp.float32) + mixing * total.astype(jnp.float32)).astype(jnp.bfloat16)


def on_device(
    states,
    targets,
    loss_mask,
    cand_of,
    lambdas,
    base_q,
    delta_q,
    base_k,
    delta_k,
    base_v,
    delta_v,
    base_o,
    delta_o,
    pre_gain,
    post_gain,
    final_gain,
    unembed,
):
    cand_id = lax.axis_index("cand")
    tensor_id = lax.axis_index("tensor")
    tensor_count = lax.axis_size("tensor")
    chosen = cand_of[cand_id]
    mixing = lambdas[chosen]
    group_size = tensor_count // KV
    head_start = tensor_id // group_size * HEAD_SIZE
    own_base_k = lax.dynamic_slice_in_dim(base_k, head_start, HEAD_SIZE, 1)
    own_base_v = lax.dynamic_slice_in_dim(base_v, head_start, HEAD_SIZE, 1)
    own_delta_k = lax.dynamic_slice_in_dim(delta_k, head_start, HEAD_SIZE, 2)
    own_delta_v = lax.dynamic_slice_in_dim(delta_v, head_start, HEAD_SIZE, 2)
    summed = [task_total(delta) for delta in (delta_q, own_delta_k, own_delta_v, delta_o)]
    pieces = (
        lax.all_gather(base_q, "cand", axis=0, tiled=True),
        lax.all_gather(own_base_k, "cand", axis=0, tiled=True),
        lax.all_gather(own_base_v, "cand", axis=0, tiled=True),
        lax.all_gather(base_o, "cand", axis=1, tiled=True),
        lax.all_gather(summed[0], "cand", axis=0, tiled=True),
        lax.all_gather(summed[1], "cand", axis=0, tiled=True),
        lax.all_gather(summed[2], "cand", axis=0, tiled=True),
        lax.all_gather(summed[3], "cand", axis=1, tiled=True),
    )
    base_parts = pieces[:4]
    task_parts = pieces[4:]
    w_query = merge_weights(base_parts[0], task_parts[0], mixing)
    w_key = merge_weights(base_parts[1], task_parts[1], mixing)
    w_value = merge_weights(base_parts[2], task_parts[2], mixing)
    w_out = merge_weights(base_parts[3], task_parts[3], mixing)
    length = states.shape[0]
    stream = states.astype(jnp.float32)
    normed = root_norm(stream, pre_gain).astype(jnp.bfloat16)
    query_rows = jnp.dot(normed, w_query, preferred_element_type=jnp.float32).reshape(
        length, -1, HEAD_SIZE
    )
    query_rows = rotate_pairs(query_rows, length).astype(jnp.bfloat16)
    key_full = jnp.dot(normed, w_key, preferred_element_type=jnp.float32).astype(jnp.bfloat16)
    value_full = jnp.dot(normed, w_value, preferred_element_type=jnp.float32).astype(jnp.bfloat16)
    key_matrix = rotate_pairs(
        key_full.astype(jnp.float32).reshape(length, 1, HEAD_SIZE), length
    ).astype(jnp.bfloat16)[:, 0, :]
    attention_scores = jnp.einsum(
        "lhd,md->hlm", query_rows, key_matrix, preferred_element_type=jnp.float32
    ) * HEAD_SIZE ** (-0.5)
    attention_scores = 50.0 * jnp.tanh(attention_scores / 50.0)
    causal = jnp.arange(length)[:, None] >= jnp.arange(length)[None, :]
    weights = jnp.where(causal[None, :, :], jnp.exp(attention_scores), 0.0)
    attention_probs = (weights / jnp.sum(weights, axis=-1, keepdims=True)).astype(jnp.bfloat16)
    context_rows = jnp.einsum(
        "hlm,md->lhd", attention_probs, value_full, preferred_element_type=jnp.float32
    )
    context_rows = context_rows.astype(jnp.bfloat16).reshape(length, -1)
    partial_value = jnp.dot(context_rows, w_out, preferred_element_type=jnp.float32)
    vocab_width = unembed.shape[1]
    vocab_start = (cand_id * tensor_count + tensor_id) * vocab_width
    vocab_index = jnp.arange(vocab_width)
    attended = lax.psum(partial_value, "tensor")
    final_rows = root_norm(stream + root_norm(attended, post_gain), final_gain).astype(jnp.bfloat16)
    logits = jnp.dot(
        lax.all_gather(final_rows, "cand", axis=0, tiled=True),
        unembed,
        preferred_element_type=jnp.float32,
    )
    capped = 30.0 * jnp.tanh(logits / 30.0)
    totals = jnp.sum(jnp.exp(capped), axis=1)
    local_ids = targets - vocab_start
    matches = local_ids[:, None] == vocab_index[None, :]
    picked = jnp.sum(jnp.where(matches, capped, 0.0), axis=1)
    vocab_sums = jnp.stack([totals, picked], axis=0)
    summed_terms = lax.psum(vocab_sums, ("cand", "tensor"))
    own_terms = lax.dynamic_slice_in_dim(summed_terms, cand_id * length, length, 1)
    mask_values = loss_mask.astype(jnp.float32)
    token_loss = mask_values * (jnp.log(own_terms[0]) - own_terms[1])
    onehot = (chosen == jnp.arange(CANDS)).astype(jnp.float32)
    loss_sums, counts = lax.psum(
        (onehot * jnp.sum(token_loss), onehot * jnp.sum(mask_values)), "cand"
    )
    return (token_loss, loss_sums / jnp.maximum(counts, 1.0))


def solution(mesh):
    in_specs = (
        P("cand", None),
        P(),
        P("cand"),
        P(),
        P(),
        P("cand", "tensor"),
        P(None, "cand", "tensor"),
        P("cand", None),
        P(None, "cand", None),
        P("cand", None),
        P(None, "cand", None),
        P("tensor", "cand"),
        P(None, "tensor", "cand"),
        P(),
        P(),
        P(),
        P(None, ("cand", "tensor")),
    )
    out_specs = (P("cand"), P())
    return jax.shard_map(
        on_device, mesh=mesh, in_specs=in_specs, out_specs=out_specs, check_vma=False
    )
```

profile of v0, /device:TPU:0, one launch (start us, length us, event | category | flops | bytes accessed | tf_op | source)
XLA Modules:
  0.0 451.5 jit_solution(439209231556427896)
XLA Ops:
  7.2 0.0 all-gather.14.cloned.1.call-start
  7.2 1.9 constant_dynamic-slice_fusion.1
  9.2 0.0 all-gather.14.cloned.1.call-update
  9.2 0.0 all-gather.16.cloned.1.call-start
  9.2 2.3 dynamic-slice_reduce_fusion
  11.5 0.0 all-gather.16.cloned.1.call-update
  11.6 0.0 all-gather.20.cloned.1.call-start
  11.6 1.6 reduce_sum.123
  13.2 0.0 all-gather.20.cloned.1.call-update
  13.2 0.0 all-gather.18.cloned.1.call-start
  13.2 0.5 all-gather.18.cloned.1.call-update
  13.8 0.0 all-gather.10.cloned.1.call-start
  13.8 1.8 constant_dynamic-slice_fusion.2
  15.7 0.0 all-gather.10.cloned.1.call-update
  15.7 0.0 copy-start.8
  15.7 0.0 all-gather.12.cloned.1.call-start
  15.7 2.4 dynamic-slice_reduce_fusion.1
  18.1 0.0 all-gather.12.cloned.1.call-update
  18.2 0.0 all-gather.24.cloned.1.call-start
  18.2 0.0 copy-done.3
  18.2 1.5 reduce_sum.125
  19.7 0.0 all-gather.24.cloned.1.call-update
  19.7 0.0 all-gather.22.cloned.1.call-start
  19.8 0.7 all-gather.22.cloned.1.call-update
  20.5 0.0 all-reduce.3.cloned.1.call-start
  20.5 0.0 copy-done.9
  20.6 0.6 dynamic_slice.22
  23.1 0.0 copy-done.10
  23.1 0.6 dynamic_slice.23
  23.7 0.3 fusion.4
  24.0 0.3 multiply_cosine_fusion
  24.3 9.1 %all-gather.14.cloned.1.call-done = bf16[3584,256]{1,0:T(8,128)(2,1)} async-done(((bf16[896,256]{1,0:T(8,128)(2,1)}), bf16[3584,256]{1,0:T(8,128)(2,1)}) %all-gather.14.cloned.1.call-update) | async-done | bytes 1835024 | tf_op jit(solution)/shard_map/all_gather | solution.py:75
  33.4 22.7 %all-gather.16.cloned.1.call-done = bf16[3584,256]{1,0:T(8,128)(2,1)} async-done(((bf16[896,256]{1,0:T(8,128)(2,1)}), bf16[3584,256]{1,0:T(8,128)(2,1)}) %all-gather.16.cloned.1.call-update) | async-done | bytes 1835024 | tf_op jit(solution)/shard_map/all_gather | solution.py:79
  56.1 3.6 fusion.20
  59.7 0.3 fusion.37
  60.0 29.2 %all-gather.20.cloned.1.call-done = bf16[3584,512]{1,0:T(8,128)(2,1)} async-done(((bf16[896,512]{1,0:T(8,128)(2,1)}), bf16[3584,512]{1,0:T(8,128)(2,1)}) %all-gather.20.cloned.1.call-update) | async-done | bytes 3670032 | tf_op jit(solution)/shard_map/all_gather | solution.py:78
  89.2 32.9 %all-gather.18.cloned.1.call-done = bf16[3584,512]{1,0:T(8,128)(2,1)} async-done(((bf16[896,512]{1,0:T(8,128)(2,1)}), bf16[3584,512]{1,0:T(8,128)(2,1)}) %all-gather.18.cloned.1.call-update) | async-done | bytes 3670032 | tf_op jit(solution)/shard_map/all_gather | solution.py:74
  122.1 5.2 %fusion = f32[128,512]{1,0:T(8,128)S(1)} fusion(bf16[3584,512]{1,0:T(8,128)(2,1)} %all-gather.20.cloned.1.call-done, bf16[3584,512]{1,0:T(8,128)(2,1)} %all-gather.18.cloned.1.call-done, f32[]{:T(128)} %bitcast.1, bf16[128,3584]{1,0:T(8,128)(2,1)S(1)} %copy-done.1, f32[3584]{0:T(1024)S(1)} %copy-done.8, f32[128]{0:T(128)S(1)} %add_rsqrt_fusion.2), kind=kOutput, calls=%fused_computation.6 | convolution fusion | flops 480772096 | bytes 8534532 | tf_op jit(solution)/shard_map/dot_general | solution.py:92
  127.3 0.2 reshape.177
  127.5 0.1 fusion.53
  127.7 0.2 fusion.15
  127.9 16.7 %all-gather.10.cloned.1.call-done = bf16[3584,256]{1,0:T(8,128)(2,1)} async-done(((bf16[896,256]{1,0:T(8,128)(2,1)}), bf16[3584,256]{1,0:T(8,128)(2,1)}) %all-gather.10.cloned.1.call-update) | async-done | bytes 1835024 | tf_op jit(solution)/shard_map/all_gather | solution.py:76
  144.6 22.5 %all-gather.12.cloned.1.call-done = bf16[3584,256]{1,0:T(8,128)(2,1)} async-done(((bf16[896,256]{1,0:T(8,128)(2,1)}), bf16[3584,256]{1,0:T(8,128)(2,1)}) %all-gather.12.cloned.1.call-update) | async-done | bytes 1835024 | tf_op jit(solution)/shard_map/all_gather | solution.py:80
  167.2 3.9 convolution_convert_fusion
  171.1 29.1 %all-gather.24.cloned.1.call-done = bf16[512,3584]{1,0:T(8,128)(2,1)} async-done(((bf16[512,896]{1,0:T(8,128)(2,1)}), bf16[512,3584]{1,0:T(8,128)(2,1)}) %all-gather.24.cloned.1.call-update) | async-done | bytes 3670032 | tf_op jit(solution)/shard_map/all_gather | solution.py:81
  200.2 33.1 %all-gather.22.cloned.1.call-done = bf16[512,3584]{1,0:T(8,128)(2,1)} async-done(((bf16[512,896]{1,0:T(8,128)(2,1)}), bf16[512,3584]{1,0:T(8,128)(2,1)}) %all-gather.22.cloned.1.call-update) | async-done | bytes 3670032 | tf_op jit(solution)/shard_map/all_gather | solution.py:77
  233.3 6.6 %fusion.1 = f32[128,3584]{1,0:T(8,128)} fusion(bf16[128,512]{0,1:T(8,128)(2,1)S(1)} %bitcast.38, bf16[512,3584]{1,0:T(8,128)(2,1)} %all-gather.24.cloned.1.call-done, bf16[512,3584]{1,0:T(8,128)(2,1)} %all-gather.22.cloned.1.call-done, f32[]{:T(128)} %bitcast.1), kind=kOutput, calls=%fused_computation.7 | convolution fusion | flops 478937088 | bytes 9306116 | tf_op jit(solution)/shard_map/dot_general | solution.py:112
  239.9 0.0 all-reduce.3.cloned.1.call-update
  239.9 0.2 all-gather.26.cloned.1.call-start
  240.2 95.7 %all-reduce.3.cloned.1.call-done = f32[128,3584]{1,0:T(8,128)} async-done(((f32[128,3584]{1,0:T(8,128)}), f32[128,3584]{1,0:T(8,128)}) %all-reduce.3.cloned.1.call-update) | async-done | bytes 1835024 | tf_op jit(solution)/shard_map/psum | solution.py:116
  335.9 1.8 multiply_reduce_fusion.1
  337.8 0.0 copy-start.6
  337.8 2.0 multiply_reduce_fusion
  339.8 1.4 multiply_convert_fusion
  341.2 0.0 all-gather.26.cloned.1.call-update
  341.2 0.0 copy-done.6
  341.3 0.0 copy-start.7
  341.3 31.1 %all-gather.26.cloned.1.call-done = bf16[512,3584]{1,0:T(8,128)(2,1)} async-done(((bf16[128,3584]{1,0:T(8,128)(2,1)}), bf16[512,3584]{1,0:T(8,128)(2,1)}) %all-gather.26.cloned.1.call-update) | async-done | bytes 3670032 | tf_op jit(solution)/shard_map/all_gather | solution.py:119
  372.4 22.9 %exponential_reduce_fusion = (f32[512]{0:T(512)S(1)}, f32[512]{0:T(512)S(1)}) fusion(s32[512]{0:T(512)S(1)} %broadcast_subtract_fusion, bf16[512,3584]{1,0:T(8,128)(2,1)} %all-gather.26.cloned.1.call-done, bf16[3584,4096]{1,0:T(8,128)(2,1)} %param.33), kind=kOutput, calls=%fused_computation.2 | convolution fusion | flops 15044968448 | bytes 33036288 | tf_op jit(solution)/shard_map/dot_general | solution.py:118
  395.3 39.3 %psum.29 = f32[2,512]{1,0:T(2,128)S(1)} all-reduce(f32[2,512]{1,0:T(2,128)S(1)} %pad_maximum_fusion), channel_id=1, replica_groups=mesh['cand'=4,'tensor'=8] {'cand','tensor'}, use_global_device_ids=true, to_apply=%region_11.12 | all-reduce | flops 1024 | bytes 8192 | tf_op jit(solution)/shard_map/psum | solution.py:129
  434.7 1.1 fusion.52
  435.8 1.8 compare_select_fusion
  437.6 6.5 %all-reduce = (f32[4]{0:T(128)S(1)}, f32[4]{0:T(128)S(1)}) all-reduce(f32[4]{0:T(128)S(1)} %get-tuple-element.18, f32[4]{0:T(128)S(1)} %get-tuple-element.17), channel_id=1, replica_groups=mesh['cand'=4,'tensor'=8] {'cand'}, use_global_device_ids=true, to_apply=%region_13.14 | all-reduce | flops 8 | bytes 64 | tf_op jit(solution)/shard_map/psum | solution.py:134
  444.2 0.5 maximum_divide_fusion
  (25 shorter events, 0.1 us)
Async XLA Ops:
  7.2 4.4 copy-start.2
  7.2 26.2 %all-gather.14.cloned.1.call-start = ((), (), s32[]{:S(2)}) async-start(), calls=%async_computation.2 | async-start | bytes 2293760 | tf_op jit(solution)/shard_map/all_gather | solution.py:75
  9.2 46.9 %all-gather.16.cloned.1.call-start = ((), (), s32[]{:S(2)}) async-start(), calls=%async_computation.3 | async-start | bytes 2293760 | tf_op jit(solution)/shard_map/all_gather | solution.py:79
  11.6 77.6 %all-gather.20.cloned.1.call-start = ((), (), s32[]{:S(2)}) async-start(), calls=%async_computation.5 | async-start | bytes 4587520 | tf_op jit(solution)/shard_map/all_gather | solution.py:78
  13.2 5.0 %copy-start.3 = (bf16[2,512,896]{2,1,0:T(8,128)(2,1)S(1)}, bf16[2,512,896]{2,1,0:T(8,128)(2,1)}, u32[]{:S(2)}) copy-start(bf16[2,512,896]{2,1,0:T(8,128)(2,1)} %param.29) | copy-start | bytes 5505028
  13.2 108.9 %all-gather.18.cloned.1.call-start = ((), (), s32[]{:S(2)}) async-start(), calls=%async_computation.4 | async-start | bytes 4587520 | tf_op jit(solution)/shard_map/all_gather | solution.py:74
  13.8 130.9 %all-gather.10.cloned.1.call-start = ((), (), s32[]{:S(2)}) async-start(), calls=%async_computation | async-start | bytes 2293760 | tf_op jit(solution)/shard_map/all_gather | solution.py:76
  15.6 4.9 %copy-start.9 = (s32[4]{0:T(128)S(1)}, s32[4]{0:T(128)}, u32[]{:S(2)}) copy-start(s32[4]{0:T(128)} %param.20) | copy-start | bytes 52
  15.6 7.4 %copy-start.10 = (f32[4]{0:T(128)S(1)}, f32[4]{0:T(128)}, u32[]{:S(2)}) copy-start(f32[4]{0:T(128)} %param.21) | copy-start | bytes 52
  15.7 8.1 %copy-start.1 = (bf16[128,3584]{1,0:T(8,128)(2,1)S(1)}, bf16[128,3584]{1,0:T(8,128)(2,1)}, u32[]{:S(2)}) copy-start(bf16[128,3584]{1,0:T(8,128)(2,1)} %param.17) | copy-start | bytes 2752516
  15.7 40.4 %copy-start.8 = (f32[3584]{0:T(1024)S(1)}, f32[3584]{0:T(1024)}, u32[]{:S(2)}) copy-start(f32[3584]{0:T(1024)} %param.30) | copy-start | bytes 43012
  15.7 151.5 %all-gather.12.cloned.1.call-start = ((), (), s32[]{:S(2)}) async-start(), calls=%async_computation.1 | async-start | bytes 2293760 | tf_op jit(solution)/shard_map/all_gather | solution.py:80
  18.2 182.1 %all-gather.24.cloned.1.call-start = ((), (), s32[]{:S(2)}) async-start(), calls=%async_computation.7 | async-start | bytes 4587520 | tf_op jit(solution)/shard_map/all_gather | solution.py:81
  19.7 213.6 %all-gather.22.cloned.1.call-start = ((), (), s32[]{:S(2)}) async-start(), calls=%async_computation.6 | async-start | bytes 4587520 | tf_op jit(solution)/shard_map/all_gather | solution.py:77
  20.5 315.4 %all-reduce.3.cloned.1.call-start = ((), (), s32[]{:S(2)}) async-start(), calls=%async_computation.8 | async-start | bytes 3670016 | tf_op jit(solution)/shard_map/psum | solution.py:116
  239.9 97.8 %copy-start.4 = (f32[3584]{0:T(1024)S(1)}, f32[3584]{0:T(1024)}, u32[]{:S(2)}) copy-start(f32[3584]{0:T(1024)} %param.31) | copy-start | bytes 43012
  239.9 99.9 %copy-start.5 = (f32[3584]{0:T(1024)S(1)}, f32[3584]{0:T(1024)}, u32[]{:S(2)}) copy-start(f32[3584]{0:T(1024)} %param.32) | copy-start | bytes 43012
  239.9 132.5 %all-gather.26.cloned.1.call-start = ((), (), s32[]{:S(2)}) async-start(), calls=%async_computation.9 | async-start | bytes 4587520 | tf_op jit(solution)/shard_map/all_gather | solution.py:119
  335.9 3.9 copy-start
  337.8 3.5 copy-start.6
  341.3 93.4 %copy-start.7 = (s32[128]{0:T(128)S(1)}, s32[128]{0:T(128)}, u32[]{:S(2)}) copy-start(s32[128]{0:T(128)} %param.19) | copy-start | bytes 1540
Sparse Core Ops, SparseCore 0:
  9.5 23.8 all-gather.13
  35.0 21.0 all-gather.15
  57.7 31.4 all-gather.19
  90.6 31.4 all-gather.17
  123.5 21.0 all-gather.9
  146.1 21.0 all-gather.11
  168.7 31.4 all-gather.23
  201.8 31.4 all-gather.21
  240.1 95.7 all-reduce.2
  341.4 30.9 all-gather.25
where the time goes:
time: 452 us
  waiting for transfers between devices  324 us (72%)
  blocking collectives  45.9 us (10%)
  matrix products  42.5 us (9%)
  other arithmetic  17.5 us (4%)
  between operations  16.3 us (4%)
  local copies, waits for them, and re-layouts  5.26 us (1%)
    psum x1, waiting for transfers between devices, on_device(): attended = lax.psum(partial_value, 'tensor')  95.7 us
    psum x1, blocking collectives, on_device(): summed_terms = lax.psum(vocab_sums, ('cand', 'tensor'))  39.3 us
    all_gather x1, waiting for transfers between devices, on_device(): lax.all_gather(base_o, 'cand', axis=1, tiled=True)  33.1 us
    all_gather x1, waiting for transfers between devices, on_device(): lax.all_gather(base_q, 'cand', axis=0, tiled=True)  32.9 us
    all_gather x1, waiting for transfers between devices, on_device(): lax.all_gather(final_rows, 'cand', axis=0, tiled=True)  31.1 us
    all_gather x1, waiting for transfers between devices, on_device(): lax.all_gather(summed[0], 'cand', axis=0, tiled=True)  29.2 us
    all_gather x1, waiting for transfers between devices, on_device(): lax.all_gather(summed[3], 'cand', axis=1, tiled=True)  29.1 us
    dot_general x1, matrix products, on_device(): jnp.dot(lax.all_gather(final_rows, 'cand', axis=0, tiled=True), unembed,...  22.9 us
  transfers between devices with their start and end apart: 10, of which 10 were waited for; matrix products, arithmetic and copies ran while one was open for 6% of the time, Pallas kernels for 0%

commit v1 on v0

v1 whole, which is shorter than its diff:
```python
import functools
import math

import jax
import jax.numpy as jnp
from jax import lax
from jax.experimental import pallas as pl
from jax.experimental.pallas import tpu as pltpu
from jax.sharding import PartitionSpec as P

KV = 8
HEAD_SIZE = 256
CANDS = 4
EPS = 1e-06
BF16 = jnp.bfloat16
F32 = jnp.float32
PARTS = 2
MIB = 1024 * 1024

VM = pl.BlockSpec(memory_space=pltpu.VMEM)
SM = pl.BlockSpec(memory_space=pltpu.SMEM)


def params(mib):
    return pltpu.CompilerParams(vmem_limit_bytes=mib * MIB)


def cost(flops, nbytes):
    return pl.CostEstimate(flops=int(flops), bytes_accessed=int(nbytes), transcendentals=0)


def shape(dims, dtype):
    return jax.ShapeDtypeStruct(tuple(dims), dtype)


def swap(value, axis, mask):
    size = lax.axis_size(axis)
    return lax.ppermute(value, axis, [(i, i ^ mask) for i in range(size)])


def swap_both(value, cand_mask, tensor_mask):
    cands, tensors = lax.axis_size("cand"), lax.axis_size("tensor")
    pairs = [
        (c * tensors + t, (c ^ cand_mask) * tensors + (t ^ tensor_mask))
        for c in range(cands)
        for t in range(tensors)
    ]
    return lax.ppermute(value, ("cand", "tensor"), pairs)


def tile_of(size, *choices):
    for choice in choices:
        if size % choice == 0:
            return choice
    return size


TAIL = 8


def cut_body(width, ids, states, *pieces):
    length = states.shape[0]
    stream = states[...].astype(F32)
    mean = jnp.mean(stream * stream, axis=-1, keepdims=True)
    rest = jnp.transpose(jnp.broadcast_to(lax.rsqrt(mean + EPS), (length, 128)))[:TAIL]
    rows = lax.broadcasted_iota(jnp.int32, (TAIL, length), 0)
    tail = jnp.zeros((TAIL, length), F32)
    for row in range(3):
        term = rest.astype(BF16).astype(F32)
        tail = jnp.where(rows == row, term, tail)
        rest = rest - term
    tail = tail.astype(BF16)
    for k, out in enumerate(pieces):
        start = pl.multiple_of((ids[0] ^ k) * width, 128)
        out[:length, :] = states[:, pl.ds(start, width)]
        out[length:, :] = jnp.zeros((TAIL, width), BF16)
        out[length:, :length] = tail


def cut_call(ids, states, cands):
    length, features = states.shape
    width = features // cands
    return pl.pallas_call(
        functools.partial(cut_body, width),
        in_specs=[SM, VM],
        out_specs=[VM] * cands,
        out_shape=[shape((length + TAIL, width), BF16)] * cands,
        compiler_params=params(8),
        cost_estimate=cost(1e9, 4 * states.size),
        name="cut",
    )(ids, states)


def cut_plain(own, states, cands):
    length, features = states.shape
    width = features // cands
    stream = states.astype(F32)
    rest = lax.rsqrt(jnp.mean(stream * stream, axis=-1) + EPS)
    terms = []
    for _ in range(3):
        term = lax.reduce_precision(rest, 8, 7)
        terms.append(term)
        rest = rest - term
    tail = jnp.pad(jnp.stack(terms), ((0, TAIL - 3), (0, width - length))).astype(BF16)
    return [
        jnp.concatenate(
            [lax.dynamic_slice_in_dim(states, (own ^ k) * width, width, 1), tail], axis=0
        )
        for k in range(cands)
    ]


def task_sum(delta):
    total = delta[0].astype(F32)
    for task in range(1, delta.shape[0]):
        total = total + delta[task].astype(F32)
    return total.astype(BF16)


def prep_body(ids, *refs):
    *ins, out = refs
    half = out.shape[1] // 2
    col = 0
    for base, delta in zip(ins[::2], ins[1::2]):
        width = base.shape[1]
        out[:, col : col + width] = base[...]
        out[:, half + col : half + col + width] = task_sum(delta)
        col += width


def prep_call(ids, pairs):
    rows = pairs[0][0].shape[0]
    tile = tile_of(rows, 128, 112, 64, 32, 16)
    specs, operands, total_width = [], [], 0
    for base, delta, width, of_head in pairs:
        at = (lambda ids: ids[1]) if of_head else (lambda ids: 0)
        specs.append(pl.BlockSpec((tile, width), lambda i, ids, at=at: (i, at(ids))))
        specs.append(
            pl.BlockSpec((delta.shape[0], tile, width), lambda i, ids, at=at: (0, i, at(ids)))
        )
        operands += [base, delta]
        total_width += width
    return pl.pallas_call(
        prep_body,
        grid_spec=pltpu.PrefetchScalarGridSpec(
            num_scalar_prefetch=1,
            grid=(rows // tile,),
            in_specs=specs,
            out_specs=pl.BlockSpec((tile, 2 * total_width), lambda i, ids: (i, 0)),
        ),
        out_shape=shape((rows, 2 * total_width), BF16),
        compiler_params=params(58),
        cost_estimate=cost(2e9, rows * total_width * 10),
        name="prep",
    )(ids, *operands)


def qkv_body(count, first, ids, cand_of, lambdas, *refs):
    pieces, gain, weights = refs[:count], refs[count], refs[count + 1]
    outs, normed = refs[count + 2 : -1], refs[-1]
    length, columns = outs[0].shape
    for k in range(count):
        turned = jnp.transpose(pieces[k][length:, :length].astype(F32))
        column = turned[:, 0:1] + turned[:, 1:2] + turned[:, 2:3]
        raw = pieces[k][:length, :].astype(F32)
        normed[k * length : (k + 1) * length, :] = (raw * column * gain[...][:1]).astype(BF16)
    chunk = tile_of(columns, 256, 128)
    for start in range(0, columns, chunk):
        base = jnp.dot(
            normed[...], weights[:, start : start + chunk], preferred_element_type=F32
        )
        task = jnp.dot(
            normed[...],
            weights[:, columns + start : columns + start + chunk],
            preferred_element_type=F32,
        )
        for k in range(count):
            mixing = lambdas[cand_of[ids[0] ^ (first + k)]]
            rows = slice(k * length, (k + 1) * length)
            outs[k][:, start : start + chunk] = base[rows] + mixing * task[rows]


def qkv_call(ids, cand_of, lambdas, pieces, gain, weights, first):
    count = len(pieces)
    length, width = pieces[0].shape[0] - TAIL, pieces[0].shape[1]
    columns = weights.shape[1] // 2
    return pl.pallas_call(
        functools.partial(qkv_body, count, first),
        in_specs=[SM] * 3 + [VM] * (count + 2),
        out_specs=[VM] * count,
        out_shape=[shape((length, columns), F32)] * count,
        scratch_shapes=[pltpu.VMEM((count * length, width), BF16)],
        compiler_params=params(16),
        cost_estimate=cost(4 * count * length * width * columns, 2 * weights.size),
        name="qkv",
    )(ids, cand_of, lambdas, *pieces, gain, weights)


def join_body(own, other, out):
    out[...] = (own[...] + other[...]).astype(BF16)


def join_call(own, other):
    return pl.pallas_call(
        join_body,
        in_specs=[VM, VM],
        out_specs=VM,
        out_shape=shape(own.shape, BF16),
        compiler_params=params(4),
        cost_estimate=cost(1e8, 10 * own.size),
        name="join",
    )(own, other)


def attend_body(n_more, heads, *refs):
    own, cosine, sine = refs[:3]
    more, out = refs[3 : 3 + n_more], refs[3 + n_more]
    length = own.shape[0]
    half = HEAD_SIZE // 2
    cos, sin = cosine[...], sine[...]

    def piece(start, width):
        total = own[:, start : start + width]
        for ref in more:
            total = total + ref[:, start : start + width].astype(F32)
        return total

    def rotate(u):
        first, second = u[:, :half], u[:, half:]
        return jnp.concatenate([first * cos - second * sin, second * cos + first * sin], axis=-1)

    q_width = heads * HEAD_SIZE
    key = rotate(piece(q_width, HEAD_SIZE).astype(BF16).astype(F32)).astype(BF16)
    value = piece(q_width + HEAD_SIZE, HEAD_SIZE).astype(BF16)
    rows = lax.broadcasted_iota(jnp.int32, (length, length), 0)
    columns = lax.broadcasted_iota(jnp.int32, (length, length), 1)
    causal = rows >= columns
    for head in range(heads):
        query = rotate(piece(head * HEAD_SIZE, HEAD_SIZE)).astype(BF16)
        score = lax.dot_general(
            query, key, (((1,), (1,)), ((), ())), preferred_element_type=F32
        ) * HEAD_SIZE ** (-0.5)
        score = 50.0 * jnp.tanh(score / 50.0)
        weight = jnp.where(causal, jnp.exp(score), 0.0)
        probs = (weight / jnp.sum(weight, axis=-1, keepdims=True)).astype(BF16)
        context = jnp.dot(probs, value, preferred_element_type=F32)
        out[:, head * HEAD_SIZE : (head + 1) * HEAD_SIZE] = context.astype(BF16)


def attend_call(own, more, cosine, sine, heads):
    length = own.shape[0]
    return pl.pallas_call(
        functools.partial(attend_body, len(more), heads),
        in_specs=[VM] * (3 + len(more)),
        out_specs=VM,
        out_shape=shape((length, heads * HEAD_SIZE), BF16),
        compiler_params=params(16),
        cost_estimate=cost(1e9, 4 * own.size),
        name="attend",
    )(own, cosine, sine, *more)


def project_body(cands, group, ids, cand_of, lambdas, *refs):
    contexts, base, task = refs[:cands], refs[cands], refs[cands + 1]
    keep, send, stack = refs[cands + 2 :]
    own, bit = ids[0], ids[1]
    half = group // 2
    length, width = keep.shape[1:]
    for k in range(cands):
        stack[k * length : (k + 1) * length, :] = contexts[k][...]
    for start in range(0, width, 256):
        cols = slice(start, min(start + 256, width))
        of_base = jnp.dot(stack[...], base[:, cols], preferred_element_type=F32)
        of_task = jnp.dot(stack[...], task[:, cols], preferred_element_type=F32)
        for k in range(cands):
            seq = own ^ k
            part, inside = seq // group, seq % group
            at = part * half + inside % half
            mixing = lambdas[cand_of[seq]]
            rows = slice(k * length, (k + 1) * length)
            result = of_base[rows] + mixing * of_task[rows]
            mine = inside // half == bit

            @pl.when(mine)
            def _():
                keep[at, :, cols] = result

            @pl.when(jnp.logical_not(mine))
            def _():
                send[at, :, cols] = result.astype(BF16)


def project_call(ids, cand_of, lambdas, contexts, base, task, group):
    cands = len(contexts)
    length, depth = contexts[0].shape
    width = base.shape[1]
    return pl.pallas_call(
        functools.partial(project_body, cands, group),
        in_specs=[SM] * 3 + [VM] * (cands + 2),
        out_specs=[VM, VM],
        out_shape=[shape((cands // 2, length, width), F32), shape((cands // 2, length, width), BF16)],
        scratch_shapes=[pltpu.VMEM((cands * length, depth), BF16)],
        compiler_params=params(24),
        cost_estimate=cost(4 * cands * length * width * depth, 4 * base.size),
        name="project",
    )(ids, cand_of, lambdas, *contexts, base, task)


def tasks_body(delta, out):
    out[...] = task_sum(delta)


def tasks_call(delta):
    tasks, rows, width = delta.shape
    tile = tile_of(rows, 128)
    return pl.pallas_call(
        tasks_body,
        grid=(rows // tile,),
        in_specs=[pl.BlockSpec((tasks, tile, width), lambda i: (0, i, 0))],
        out_specs=pl.BlockSpec((tile, width), lambda i: (i, 0)),
        out_shape=shape((rows, width), BF16),
        compiler_params=params(16),
        cost_estimate=cost(1e9, 6 * rows * width),
        name="tasks",
    )(delta)


def spread_body(blocks, rows, ids, keep, got, own, *sends):
    at = ids[2]
    for mask in range(blocks):
        start = pl.multiple_of((at ^ mask) * rows, rows)
        total = keep[pl.ds(start, rows), :] + got[pl.ds(start, rows), :].astype(F32)
        if mask == 0:
            own[...] = total
        else:
            sends[mask - 1][...] = total.astype(BF16)


def spread_call(ids, keep, got, blocks):
    rows, width = keep.shape[0] // blocks, keep.shape[1]
    return pl.pallas_call(
        functools.partial(spread_body, blocks, rows),
        in_specs=[SM, VM, VM],
        out_specs=[VM] * blocks,
        out_shape=[shape((rows, width), F32)] + [shape((rows, width), BF16)] * (blocks - 1),
        compiler_params=params(8),
        cost_estimate=cost(1e9, 8 * keep.size),
        name="spread",
    )(ids, keep, got)


def sums_body(n_got, n_raw, rows, ids, own, gain, *refs):
    got, raw = refs[:n_got], refs[n_got : n_got + n_raw]
    attended, stream, sums = refs[n_got + n_raw :]
    a = own[...]
    for ref in got:
        a = a + ref[...].astype(F32)
    attended[...] = a
    take = min(rows, raw[0].shape[0] - TAIL)
    for step in range(rows // take):
        for k in range(n_raw):

            @pl.when(ids[step] == k)
            def _():
                start = pl.multiple_of(ids[rows // take], take)
                stream[step * take : (step + 1) * take, :] = raw[k][pl.ds(start, take), :]

    s = stream[...].astype(F32)
    ag = a * gain[...][:1]
    lanes = lax.broadcasted_iota(jnp.int32, sums.shape, 1)
    total = jnp.zeros(sums.shape, F32)
    for lane, term in enumerate((a * a, s * s, s * ag, ag * ag)):
        total = jnp.where(lanes == lane, jnp.sum(term, axis=1, keepdims=True), total)
    sums[...] = total


def sums_call(ids, own, got, raw, gain):
    rows, width = own.shape
    return pl.pallas_call(
        functools.partial(sums_body, len(got), len(raw), rows),
        in_specs=[SM] + [VM] * (2 + len(got) + len(raw)),
        out_specs=[VM] * 3,
        out_shape=[shape((rows, width), F32), shape((rows, width), BF16), shape((rows, 128), F32)],
        compiler_params=params(8),
        cost_estimate=cost(1e9, 8 * own.size),
        name="sums",
    )(ids, own, gain, *got, *raw)


def finish_body(features, n_sums, attended, stream, post, final, *refs):
    sums, out = refs[:n_sums], refs[n_sums]
    total = sums[0][...]
    for ref in sums[1:]:
        total = total + ref[...]
    aa, ss, sag, agag = (total[:, i : i + 1] / features for i in range(4))
    first = lax.rsqrt(aa + EPS)
    second = lax.rsqrt(ss + 2.0 * first * sag + first * first * agag + EPS)
    mixed = stream[...].astype(F32) + attended[...] * first * post[...][:1]
    out[...] = (mixed * second * final[...][:1]).astype(BF16)


def finish_call(attended, stream, post, final, sums, features):
    return pl.pallas_call(
        functools.partial(finish_body, features, len(sums)),
        in_specs=[VM] * (4 + len(sums)),
        out_specs=VM,
        out_shape=shape(attended.shape, BF16),
        compiler_params=params(8),
        cost_estimate=cost(1e9, 8 * attended.size),
        name="finish",
    )(attended, stream, post, final, *sums)


def vocab_body(n_pieces, blocks, rows, width, at, targets, *refs):
    pieces = refs[:n_pieces]
    unembed, out, x, sem, acc = refs[n_pieces : n_pieces + 5]
    step = pl.program_id(0)

    def copies():
        for p in range(n_pieces):
            for m in range(blocks):
                row = pl.multiple_of(at[p * (blocks + 1) + 1 + m] * rows, rows)
                col = pl.multiple_of(at[p * (blocks + 1)] * width, 128)
                yield pltpu.make_async_copy(
                    pieces[p].at[pl.ds(m * rows, rows), :],
                    x.at[pl.ds(row, rows), pl.ds(col, width)],
                    sem.at[p * blocks + m],
                )

    @pl.when(step == 0)
    def _():
        for copy in copies():
            copy.start()
        acc[...] = jnp.zeros_like(acc)
        for copy in copies():
            copy.wait()

    vocab_tile(step, targets, x, unembed, out, acc)


def vocab_tile(step, targets, x, unembed, out, acc):
    rows, tile = x.shape[0], unembed.shape[1]
    sub = tile_of(tile, 256, 128)
    local = targets[...] - step * tile
    columns = lax.broadcasted_iota(jnp.int32, (rows, 128), 1)
    totals = jnp.zeros((rows, 128), F32)
    picked = jnp.zeros((rows, 128), F32)
    for start in range(0, tile, sub):
        logits = jnp.dot(
            x[...], unembed[:, start : start + sub], preferred_element_type=F32
        )
        for lane in range(0, sub, 128):
            capped = 30.0 * jnp.tanh(logits[:, lane : lane + 128] / 30.0)
            totals += jnp.exp(capped)
            picked += jnp.where(columns == local - (start + lane), capped, 0.0)
    acc[:, :128] += totals
    acc[:, 128:] += picked

    @pl.when(step == pl.num_programs(0) - 1)
    def _():
        for row in range(2):
            turned = jnp.transpose(acc[:, row * 128 : (row + 1) * 128])
            out[row : row + 1, :] = jnp.sum(turned, axis=0, keepdims=True)


def vocab_plain_body(targets, x, unembed, out, acc):
    step = pl.program_id(0)

    @pl.when(step == 0)
    def _():
        acc[...] = jnp.zeros_like(acc)

    vocab_tile(step, targets, x, unembed, out, acc)


def vocab_call(pieces, places, targets, unembed, blocks):
    rows, width = pieces[0].shape[0] // blocks, pieces[0].shape[1]
    total_rows = targets.shape[0]
    features, vocab = unembed.shape
    tile = tile_of(vocab, 1024, 512, 256, 128)
    spec = dict(
        out_shape=shape((8, total_rows), F32),
        compiler_params=params(40),
        cost_estimate=cost(2 * total_rows * features * vocab, 2 * unembed.size),
        name="vocab",
    )
    if width % 128 == 0:
        full = pl.BlockSpec((8, total_rows), lambda i, *_: (0, 0))
        return pl.pallas_call(
            functools.partial(vocab_body, len(pieces), blocks, rows, width),
            grid_spec=pltpu.PrefetchScalarGridSpec(
                num_scalar_prefetch=1,
                grid=(vocab // tile,),
                in_specs=[pl.BlockSpec((total_rows, 1), lambda i, *_: (0, 0))]
                + [pl.BlockSpec(memory_space=pl.ANY)] * len(pieces)
                + [pl.BlockSpec((features, tile), lambda i, *_: (0, i))],
                out_specs=full,
                scratch_shapes=[
                    pltpu.VMEM((total_rows, features), BF16),
                    pltpu.SemaphoreType.DMA((len(pieces) * blocks,)),
                    pltpu.VMEM((total_rows, 256), F32),
                ],
            ),
            **spec,
        )(jnp.concatenate(places).astype(jnp.int32), targets, *pieces, unembed)
    x = jnp.zeros((total_rows, features), BF16)
    for piece, place in zip(pieces, places):
        for m in range(blocks):
            x = lax.dynamic_update_slice(
                x, piece[m * rows : (m + 1) * rows], (place[1 + m] * rows, place[0] * width)
            )
    return pl.pallas_call(
        vocab_plain_body,
        grid=(vocab // tile,),
        in_specs=[
            pl.BlockSpec((total_rows, 1), lambda i: (0, 0)),
            pl.BlockSpec((total_rows, features), lambda i: (0, 0)),
            pl.BlockSpec((features, tile), lambda i: (0, i)),
        ],
        out_specs=pl.BlockSpec((8, total_rows), lambda i: (0, 0)),
        scratch_shapes=[pltpu.VMEM((total_rows, 256), F32)],
        **spec,
    )(targets, x, unembed)


def on_device(
    states,
    targets,
    loss_mask,
    cand_of,
    lambdas,
    base_q,
    delta_q,
    base_k,
    delta_k,
    base_v,
    delta_v,
    base_o,
    delta_o,
    pre_gain,
    post_gain,
    final_gain,
    unembed,
):
    cands, tensors = lax.axis_size("cand"), lax.axis_size("tensor")
    own, place = lax.axis_index("cand"), lax.axis_index("tensor")
    length, features = states.shape
    width = features // cands
    tokens = cands * length
    heads = base_q.shape[1] // HEAD_SIZE
    blocks = tensors // 2
    bit, block = place % 2, place // 2
    head = place // (tensors // KV)

    ids = jnp.stack([own, head]).astype(jnp.int32)
    aligned = width % 128 == 0 and length == 128
    cuts = cut_call(ids, states, cands) if aligned else cut_plain(own, states, cands)
    xs = [cuts[0]] + [None] * (cands - 1)
    for k in [*range(2, cands), 1]:
        xs[k] = swap(cuts[k], "cand", k)

    weights = prep_call(
        ids,
        [
            (base_q, delta_q, base_q.shape[1], False),
            (base_k, delta_k, HEAD_SIZE, True),
            (base_v, delta_v, HEAD_SIZE, True),
        ],
    )
    task_o = tasks_call(delta_o)

    gains = jnp.stack([pre_gain, post_gain, final_gain])
    gains = lax.dynamic_slice_in_dim(gains, own * width, width, 1)
    gain, post, final = (jnp.broadcast_to(gains[i : i + 1], (8, width)) for i in range(3))
    partials = []
    for first in range(0, cands, 2):
        partials += qkv_call(
            ids, cand_of, lambdas, xs[first : first + 2], gain, weights, first
        )
    crossed = [swap(partials[k + 1], "cand", 1) for k in range(0, cands, 2)]
    more = [crossed[0]]
    for k in range(2, cands, 2):
        more.append(swap(join_call(partials[k], crossed[k // 2]), "cand", k))

    positions = jnp.arange(length).astype(F32)
    half = HEAD_SIZE // 2
    frequency = jnp.exp(-math.log(10000.0) * jnp.arange(half).astype(F32) * 2.0 / HEAD_SIZE)
    angles = positions[:, None] * frequency[None, :]
    context = attend_call(partials[0], more, jnp.cos(angles), jnp.sin(angles), heads)

    contexts = [None] * cands
    contexts[0] = context
    for k in range(2, cands, 2):
        contexts[k] = swap(context, "cand", k)
    for k in range(0, cands, 2):
        contexts[k + 1] = swap(contexts[k], "cand", 1)

    group = cands // PARTS
    keep, send = project_call(
        jnp.stack([own, bit]).astype(jnp.int32), cand_of, lambdas, contexts, base_o, task_o, group
    )
    part_rows = tokens // PARTS
    rows = part_rows // tensors
    spot = jnp.stack([own, bit, block]).astype(jnp.int32)
    arrived, results = [], []
    for part in range(PARTS):
        lo, hi = part * group // 2, (part + 1) * group // 2
        got = swap(send[lo:hi], "tensor", 1).reshape(part_rows // 2, width)
        mine, *sends = spread_call(spot, keep[lo:hi].reshape(part_rows // 2, width), got, blocks)
        got = [swap(sends[m - 1], "tensor", 2 * m) for m in range(1, blocks)]
        first_row = part * part_rows + (bit * blocks + block) * rows
        where = jnp.stack(
            [(first_row // length + i) ^ own for i in range(max(1, rows // length))]
            + [first_row % length]
        ).astype(jnp.int32)
        attended, s, sums = sums_call(where, mine, got, xs, post)
        every = [sums] + [swap(sums, "cand", k) for k in range(1, cands)]
        final_rows = finish_call(attended, s, post, final, every, features)
        pile = [final_rows] + [swap(final_rows, "tensor", 2 * m) for m in range(1, blocks)]
        pile = jnp.concatenate(pile, axis=0)
        crossing = []
        for cand_mask in range(0, cands, 2):
            for bit_mask in range(2):
                moved = cand_mask or bit_mask
                crossing.append(swap_both(pile, cand_mask, bit_mask) if moved else pile)
        arrived.append(crossing)
    for part in range(PARTS):
        crossing = arrived[part]
        if part > 0:
            crossing, results[-1] = lax.optimization_barrier((crossing, results[-1]))
        pieces, places = [], []
        for index, piece in enumerate(crossing):
            cand_mask, bit_mask = index // 2 * 2, index % 2
            for core_mask in range(2):
                pieces.append(swap(piece, "cand", 1) if core_mask else piece)
                places.append(
                    jnp.stack(
                        [own ^ cand_mask ^ core_mask]
                        + [(bit ^ bit_mask) * blocks + (block ^ m) for m in range(blocks)]
                    )
                )
        vocab_start = (own * tensors + place) * unembed.shape[1]
        ids_here = targets[part * part_rows : (part + 1) * part_rows] - vocab_start
        results.append(
            vocab_call(pieces, places, ids_here.reshape(part_rows, 1), unembed, blocks)
        )
    both = jnp.concatenate(results, axis=1)[:2]
    masks = jnp.where(
        (lax.broadcasted_iota(jnp.int32, (cands, 1), 0) == own) & (place == 0),
        loss_mask.astype(F32)[None, :],
        0.0,
    ).reshape(1, tokens)
    payload = jnp.concatenate([both, masks], axis=0)
    payload = jnp.broadcast_to(payload[None], (cands * tensors,) + payload.shape)
    summed = jnp.sum(lax.all_to_all(payload, ("cand", "tensor"), 0, 0), axis=0)
    mask_values = summed[2]
    losses = mask_values * (jnp.log(summed[0]) - summed[1])
    token_loss = lax.dynamic_slice_in_dim(losses, own * length, length, 0)
    onehot = (cand_of[:, None] == jnp.arange(CANDS)[None, :]).astype(F32)
    loss_sums = jnp.sum(onehot * jnp.sum(losses.reshape(cands, length), axis=1)[:, None], axis=0)
    counts = jnp.sum(onehot * jnp.sum(mask_values.reshape(cands, length), axis=1)[:, None], axis=0)
    return (token_loss, loss_sums / jnp.maximum(counts, 1.0))


def solution(mesh):
    in_specs = (
        P("cand", None),
        P(),
        P("cand"),
        P(),
        P(),
        P("cand", "tensor"),
        P(None, "cand", "tensor"),
        P("cand", None),
        P(None, "cand", None),
        P("cand", None),
        P(None, "cand", None),
        P("tensor", "cand"),
        P(None, "tensor", "cand"),
        P(),
        P(),
        P(),
        P(None, ("cand", "tensor")),
    )
    out_specs = (P("cand"), P())
    return jax.shard_map(
        on_device, mesh=mesh, in_specs=in_specs, out_specs=out_specs, check_vma=False
    )
```

time: 452 us -> 157 us (0.35)
  waiting for transfers between devices: 324 us -> 53.8 us
  Pallas kernels: 0 us -> 49.5 us
  blocking collectives: 45.9 us -> 0 us
  matrix products: 42.5 us -> 0 us
  starting transfers between devices: 0.59 us -> 41.5 us
  between operations: 16.3 us -> 1.05 us
  other arithmetic: 17.5 us -> 2.28 us
    all_gather x9 -> x0, waiting for transfers between devices: 226 us -> none  [the longest x1 33.1 us: on_device(): lax.all_gather(base_o, 'cand', axis=1, tiled=True)]
    psum x1 -> x0, waiting for transfers between devices: 95.7 us -> none  [on_device(): attended = lax.psum(partial_value, 'tensor')]
    pallas_call x0 -> x16, Pallas kernels: none -> 49.5 us  [the longest x2 29.8 us: vocab_call(): pl.pallas_call(functools.partial(vocab_body, len(pieces), blocks, rows, w...]
    psum x2 -> x0, blocking collectives: 45.9 us -> none  [the longest x1 39.3 us: on_device(): summed_terms = lax.psum(vocab_sums, ('cand', 'tensor'))]
    ppermute x0 -> x43, waiting for transfers between devices: none -> 43.3 us  [the longest x37 43.3 us: swap(): return lax.ppermute(value, axis, [(i, i ^ mask) for i in range(size)])]
    dot_general x6 -> x0, matrix products: 42.5 us -> none  [the longest x1 22.9 us: on_device(): jnp.dot(lax.all_gather(final_rows, 'cand', axis=0, tiled=True), unembed,...]
    ppermute x0 -> x43, starting transfers between devices: none -> 39 us  [the longest x37 31.9 us: swap(): return lax.ppermute(value, axis, [(i, i ^ mask) for i in range(size)])]
    reduce_sum x8 -> x3, other arithmetic: 13 us -> 0.3 us  [the longest x1 0.14 us: on_device(): jnp.sum(mask_values.reshape(cands, length), axis=1)[:, None]]
  transfers between devices with their start and end apart: 10 -> 44, of which waited for: 10 -> 19; matrix products, arithmetic and copies ran while one was open for 6% -> 1% of each run, Pallas kernels for 0% -> 18%
where the time goes in v1:
time: 157 us
  waiting for transfers between devices  53.8 us (34%)
  Pallas kernels  49.5 us (32%)
  starting transfers between devices  41.5 us (26%)
  local copies, waits for them, and re-layouts  8.54 us (5%)
  other arithmetic  2.28 us (1%)
    ppermute x37, waiting for transfers between devices, swap(): return lax.ppermute(value, axis, [(i, i ^ mask) for i in range(size)])  43.3 us
    ppermute x37, starting transfers between devices, swap(): return lax.ppermute(value, axis, [(i, i ^ mask) for i in range(size)])  31.9 us
    pallas_call x2, Pallas kernels, vocab_call(): pl.pallas_call(functools.partial(vocab_body, len(pieces), blocks, rows, w...  29.8 us
    all_to_all x1, waiting for transfers between devices, on_device(): summed = jnp.sum(lax.all_to_all(payload, ('cand', 'tensor'), 0, 0), axis=0)  10.4 us
    pallas_call x1, Pallas kernels, prep_call(): pl.pallas_call(prep_body, grid_spec=pltpu.PrefetchScalarGridSpec(num_scal...  7.41 us
    unnamed x32, local copies, waits for them, and re-layouts  7.23 us
    ppermute x6, starting transfers between devices, swap_both(): return lax.ppermute(value, ('cand', 'tensor'), pairs)  7.11 us
    pallas_call x2, Pallas kernels, qkv_call(): pl.pallas_call(functools.partial(qkv_body, count, first), in_specs=[SM] *...  4.19 us
  transfers between devices with their start and end apart: 44, of which 19 were waited for; matrix products, arithmetic and copies ran while one was open for 1% of the time, Pallas kernels for 18%

profile of v1, /device:TPU:0, one launch (start us, length us, event | category | flops | bytes accessed | tf_op | source)
XLA Modules:
  0.0 156.7 jit_solution(8729784072337445911)
XLA Ops:
  0.7 1.2 copy-done.7
  1.9 0.9 cut.1
  2.8 3.0 %collective-permute-start.2 = (bf16[136,896]{1,0:T(8,128)(2,1)S(1)}, bf16[136,896]{1,0:T(8,128)(2,1)S(1)}, u32[]{:S(2)}, u32[]{:S(2)}) collective-permute-start(bf16[136,896]{1,0:T(8,128)(2,1)S(1)} %get-tuple-element.35), channel_id=1, source_target_pairs={{0,16},{8,24},{16,0},{24,8},{1,17},{9,25},{17,1},{25,9},{2,18},{10... | collective-permute-start | bytes 731144 | tf_op jit(solution)/shard_map/ppermute | solution.py:38
  6.0 7.4 %prep.1.refs_3_ = bf16[896,2048]{1,0:T(8,128)(2,1)} custom-call(s32[2]{0:T(128)} %copy-done.3, bf16[896,512]{1,0:T(8,128)(2,1)} %refs_0_.1, bf16[2,896,512]{2,1,0:T(8,128)(2,1)} %refs_1_.1, bf16[896,2048]{1,0:T(8,128)(2,1)} %refs_2_.1, bf16[2,896,2048]{2,1,0:T(8,128)(2,1)} %refs_3_.1, bf16[896,2048]{1,0:T(8,128)(2,1)} %refs_4_.2, bf16[2,896,2048]{2,1,0:T(8,128)(2,1)} %refs_5_.1), custom_call_target="tpu_custom_call" | custom-call | flops 2000000000 | bytes 9175040 | tf_op jit(solution)/shard_map/prep/pallas_call | solution.py:143
  13.5 2.7 %collective-permute-done.3.refs_1_.refs_6_ = bf16[136,896]{1,0:T(8,128)(2,1)S(1)} collective-permute-done((bf16[136,896]{1,0:T(8,128)(2,1)S(1)}, bf16[136,896]{1,0:T(8,128)(2,1)S(1)}, u32[]{:S(2)}, u32[]{:S(2)}) %collective-permute-start.3) | collective-permute-done | bytes 243744 | tf_op jit(solution)/shard_map/ppermute | solution.py:38
  16.2 2.0 %copy-done = bf16[896,2048]{1,0:T(8,128)(2,1)S(1)} copy-done((bf16[896,2048]{1,0:T(8,128)(2,1)S(1)}, bf16[896,2048]{1,0:T(8,128)(2,1)}, u32[]{:S(2)}) %copy-start) | copy-done | bytes 3670040
  18.2 0.7 copy-done.4
  18.9 2.1 %qkv.3 = (f32[128,1024]{1,0:T(8,128)S(1)}, f32[128,1024]{1,0:T(8,128)S(1)}) custom-call(s32[2]{0:T(128)S(1)} %copy-done.4, s32[4]{0:T(128)S(1)} %copy-done.2, f32[4]{0:T(128)S(1)} %copy-done.5, bf16[136,896]{1,0:T(8,128)(2,1)S(1)} %collective-permute-done.2.refs_0_.refs_5_, bf16[136,896]{1,0:T(8,128)(2,1)S(1)} %collective-permute-done.3.refs_1_.refs_6_, ...), custom_call_target="tpu_custom_call" | custom-call | flops 939524096 | bytes 3670016 | tf_op jit(solution)/shard_map/qkv/pallas_call | solution.py:187
  21.0 0.6 collective-permute-start.4
  21.7 1.8 %collective-permute-done.refs_1_.refs_4_ = bf16[136,896]{1,0:T(8,128)(2,1)S(1)} collective-permute-done((bf16[136,896]{1,0:T(8,128)(2,1)S(1)}, bf16[136,896]{1,0:T(8,128)(2,1)S(1)}, u32[]{:S(2)}, u32[]{:S(2)}) %collective-permute-start) | collective-permute-done | bytes 243744 | tf_op jit(solution)/shard_map/ppermute | solution.py:38
  23.5 2.1 %qkv.2 = (f32[128,1024]{1,0:T(8,128)S(1)}, f32[128,1024]{1,0:T(8,128)S(1)}) custom-call(s32[2]{0:T(128)S(1)} %copy-done.4, s32[4]{0:T(128)S(1)} %copy-done.2, f32[4]{0:T(128)S(1)} %copy-done.5, bf16[136,896]{1,0:T(8,128)(2,1)S(1)} %get-tuple-element.31.refs_0_.refs_3_, bf16[136,896]{1,0:T(8,128)(2,1)S(1)} %collective-permute-done.refs_1_.refs_4_, ...), custom_call_target="tpu_custom_call" | custom-call | flops 939524096 | bytes 3670016 | tf_op jit(solution)/shard_map/qkv/pallas_call | solution.py:187
  25.6 0.4 collective-permute-start.1
  26.1 1.8 %collective-permute-start.5 = (bf16[128,1024]{1,0:T(8,128)(2,1)S(1)}, bf16[128,1024]{1,0:T(8,128)(2,1)S(1)}, u32[]{:S(2)}, u32[]{:S(2)}) collective-permute-start(bf16[128,1024]{1,0:T(8,128)(2,1)S(1)} %join.1), channel_id=1, source_target_pairs={{0,16},{8,24},{16,0},{24,8},{1,17},{9,25},{17,1},{25,9},{2,18},{10... | collective-permute-start | bytes 786440 | tf_op jit(solution)/shard_map/ppermute | solution.py:38
  28.3 6.3 %collective-permute-done.5.refs_4_ = bf16[128,1024]{1,0:T(8,128)(2,1)S(1)} collective-permute-done((bf16[128,1024]{1,0:T(8,128)(2,1)S(1)}, bf16[128,1024]{1,0:T(8,128)(2,1)S(1)}, u32[]{:S(2)}, u32[]{:S(2)}) %collective-permute-start.5) | collective-permute-done | bytes 262176 | tf_op jit(solution)/shard_map/ppermute | solution.py:38
  34.5 0.7 attend.1.refs_0_
  35.2 1.8 %collective-permute-start.7 = (bf16[128,512]{1,0:T(8,128)(2,1)S(1)}, bf16[128,512]{1,0:T(8,128)(2,1)S(1)}, u32[]{:S(2)}, u32[]{:S(2)}) collective-permute-start(bf16[128,512]{1,0:T(8,128)(2,1)S(1)} %attend.1.refs_0_), channel_id=1, source_target_pairs={{0,16},{8,24},{16,0},{24,8},{1,17},{9,25},{17,1},{25,9},{2,18},{10... | collective-permute-start | bytes 393224 | tf_op jit(solution)/shard_map/ppermute | solution.py:38
  37.1 3.1 %collective-permute-done.7.refs_2_ = bf16[128,512]{1,0:T(8,128)(2,1)S(1)} collective-permute-done((bf16[128,512]{1,0:T(8,128)(2,1)S(1)}, bf16[128,512]{1,0:T(8,128)(2,1)S(1)}, u32[]{:S(2)}, u32[]{:S(2)}) %collective-permute-start.7) | collective-permute-done | bytes 131104 | tf_op jit(solution)/shard_map/ppermute | solution.py:38
  40.2 0.5 tasks.1.refs_5_
  40.7 1.0 copy-done.9
  41.7 1.2 copy-done.8
  42.9 1.2 copy-done.10
  44.1 2.9 %project.1 = (f32[2,128,896]{2,1,0:T(8,128)S(1)}, bf16[2,128,896]{2,1,0:T(8,128)(2,1)S(1)}) custom-call(s32[2]{0:T(128)S(1)} %pad_add_fusion.2.ids, s32[4]{0:T(128)S(1)} %copy-done.2, f32[4]{0:T(128)S(1)} %copy-done.5, bf16[128,512]{1,0:T(8,128)(2,1)S(1)} %attend.1.refs_0_, bf16[128,512]{1,0:T(8,128)(2,1)S(1)} %collective-permute-done.6.refs_1_, ...), custom_call_target="tpu_custom_call" | custom-call | flops 939524096 | bytes 1835008 | tf_op jit(solution)/shard_map/project/pallas_call | solution.py:297
  47.0 1.8 %collective-permute-start.22 = (bf16[1,128,896]{2,1,0:T(8,128)(2,1)S(1)}, bf16[1,128,896]{2,1,0:T(8,128)(2,1)S(1)}, u32[]{:S(2)}, u32[]{:S(2)}) collective-permute-start(bf16[1,128,896]{2,1,0:T(8,128)(2,1)S(1)} %get-tuple-element.69), channel_id=1, source_target_pairs={{0,1},{1,0},{2,3},{3,2},{4,5},{5,4},{6,7},{7,6},{8,9},{9,8},{10,11... | collective-permute-start | bytes 688136 | tf_op jit(solution)/shard_map/ppermute | solution.py:38
  48.9 6.2 %collective-permute-done.22 = bf16[1,128,896]{2,1,0:T(8,128)(2,1)S(1)} collective-permute-done((bf16[1,128,896]{2,1,0:T(8,128)(2,1)S(1)}, bf16[1,128,896]{2,1,0:T(8,128)(2,1)S(1)}, u32[]{:S(2)}, u32[]{:S(2)}) %collective-permute-start.22) | collective-permute-done | bytes 229408 | tf_op jit(solution)/shard_map/ppermute | solution.py:38
  55.1 0.6 spread.3
  55.7 1.9 %collective-permute-start.23 = (bf16[32,896]{1,0:T(8,128)(2,1)S(1)}, bf16[32,896]{1,0:T(8,128)(2,1)S(1)}, u32[]{:S(2)}, u32[]{:S(2)}) collective-permute-start(bf16[32,896]{1,0:T(8,128)(2,1)S(1)} %get-tuple-element.49), channel_id=1, source_target_pairs={{0,2},{1,3},{2,0},{3,1},{4,6},{5,7},{6,4},{7,5},{8,10},{9,11},{10,... | collective-permute-start | bytes 172040 | tf_op jit(solution)/shard_map/ppermute | solution.py:38
  57.6 2.6 %collective-permute-start.24 = (bf16[32,896]{1,0:T(8,128)(2,1)S(1)}, bf16[32,896]{1,0:T(8,128)(2,1)S(1)}, u32[]{:S(2)}, u32[]{:S(2)}) collective-permute-start(bf16[32,896]{1,0:T(8,128)(2,1)S(1)} %get-tuple-element.50), channel_id=1, source_target_pairs={{0,4},{1,5},{2,6},{3,7},{4,0},{5,1},{6,2},{7,3},{8,12},{9,13},{10,... | collective-permute-start | bytes 172040 | tf_op jit(solution)/shard_map/ppermute | solution.py:38
  60.3 1.7 %collective-permute-start.9 = (bf16[1,128,896]{2,1,0:T(8,128)(2,1)S(1)}, bf16[1,128,896]{2,1,0:T(8,128)(2,1)S(1)}, u32[]{:S(2)}, u32[]{:S(2)}) collective-permute-start(bf16[1,128,896]{2,1,0:T(8,128)(2,1)S(1)} %get-tuple-element.70), channel_id=1, source_target_pairs={{0,1},{1,0},{2,3},{3,2},{4,5},{5,4},{6,7},{7,6},{8,9},{9,8},{10,11... | collective-permute-start | bytes 688136 | tf_op jit(solution)/shard_map/ppermute | solution.py:38
  62.0 1.7 %collective-permute-done.24.refs_1_ = bf16[32,896]{1,0:T(8,128)(2,1)S(1)} collective-permute-done((bf16[32,896]{1,0:T(8,128)(2,1)S(1)}, bf16[32,896]{1,0:T(8,128)(2,1)S(1)}, u32[]{:S(2)}, u32[]{:S(2)}) %collective-permute-start.24) | collective-permute-done | bytes 57376 | tf_op jit(solution)/shard_map/ppermute | solution.py:38
  63.6 2.5 %collective-permute-done.25.refs_2_ = bf16[32,896]{1,0:T(8,128)(2,1)S(1)} collective-permute-done((bf16[32,896]{1,0:T(8,128)(2,1)S(1)}, bf16[32,896]{1,0:T(8,128)(2,1)S(1)}, u32[]{:S(2)}, u32[]{:S(2)}) %collective-permute-start.25) | collective-permute-done | bytes 57376 | tf_op jit(solution)/shard_map/ppermute | solution.py:38
  66.2 0.7 sums.3
  67.0 1.6 %collective-permute-start.27 = (f32[32,128]{1,0:T(8,128)S(1)}, f32[32,128]{1,0:T(8,128)S(1)}, u32[]{:S(2)}, u32[]{:S(2)}) collective-permute-start(f32[32,128]{1,0:T(8,128)S(1)} %get-tuple-element.54.refs_0_), channel_id=1, source_target_pairs={{0,16},{8,24},{16,0},{24,8},{1,17},{9,25},{17,1},{25,9},{2,18},{10... | collective-permute-start | bytes 49160 | tf_op jit(solution)/shard_map/ppermute | solution.py:38
  68.9 1.9 %collective-permute-done.27.refs_2_ = f32[32,128]{1,0:T(8,128)S(1)} collective-permute-done((f32[32,128]{1,0:T(8,128)S(1)}, f32[32,128]{1,0:T(8,128)S(1)}, u32[]{:S(2)}, u32[]{:S(2)}) %collective-permute-start.27) | collective-permute-done | bytes 16416 | tf_op jit(solution)/shard_map/ppermute | solution.py:38
  70.8 0.9 collective-permute-done.28.refs_3_
  72.0 1.7 %collective-permute-start.30 = (bf16[32,896]{1,0:T(8,128)(2,1)S(1)}, bf16[32,896]{1,0:T(8,128)(2,1)S(1)}, u32[]{:S(2)}, u32[]{:S(2)}) collective-permute-start(bf16[32,896]{1,0:T(8,128)(2,1)S(1)} %finish.3), channel_id=1, source_target_pairs={{0,4},{1,5},{2,6},{3,7},{4,0},{5,1},{6,2},{7,3},{8,12},{9,13},{10,... | collective-permute-start | bytes 172040 | tf_op jit(solution)/shard_map/ppermute | solution.py:38
  73.7 2.7 %collective-permute-start.31 = (bf16[32,896]{1,0:T(8,128)(2,1)S(1)}, bf16[32,896]{1,0:T(8,128)(2,1)S(1)}, u32[]{:S(2)}, u32[]{:S(2)}) collective-permute-start(bf16[32,896]{1,0:T(8,128)(2,1)S(1)} %finish.3), channel_id=1, source_target_pairs={{0,6},{1,7},{2,4},{3,5},{4,2},{5,3},{6,0},{7,1},{8,14},{9,15},{10,... | collective-permute-start | bytes 172040 | tf_op jit(solution)/shard_map/ppermute | solution.py:38
  76.4 0.6 spread.2
  77.1 1.7 %collective-permute-start.11 = (bf16[32,896]{1,0:T(8,128)(2,1)S(1)}, bf16[32,896]{1,0:T(8,128)(2,1)S(1)}, u32[]{:S(2)}, u32[]{:S(2)}) collective-permute-start(bf16[32,896]{1,0:T(8,128)(2,1)S(1)} %get-tuple-element.43), channel_id=1, source_target_pairs={{0,4},{1,5},{2,6},{3,7},{4,0},{5,1},{6,2},{7,3},{8,12},{9,13},{10,... | collective-permute-start | bytes 172040 | tf_op jit(solution)/shard_map/ppermute | solution.py:38
  78.7 2.7 %collective-permute-start.12 = (bf16[32,896]{1,0:T(8,128)(2,1)S(1)}, bf16[32,896]{1,0:T(8,128)(2,1)S(1)}, u32[]{:S(2)}, u32[]{:S(2)}) collective-permute-start(bf16[32,896]{1,0:T(8,128)(2,1)S(1)} %get-tuple-element.44), channel_id=1, source_target_pairs={{0,6},{1,7},{2,4},{3,5},{4,2},{5,3},{6,0},{7,1},{8,14},{9,15},{10,... | collective-permute-start | bytes 172040 | tf_op jit(solution)/shard_map/ppermute | solution.py:38
  81.5 1.5 collective-permute-start.33
  83.0 0.7 collective-permute-start.35
  83.7 1.3 collective-permute-start.37
  85.1 0.9 sums.2
  86.1 0.7 collective-permute-start.14
  86.8 0.4 collective-permute-done.13.refs_1_
  87.2 0.7 collective-permute-start.15
  87.9 6.3 %collective-permute-done.14.refs_2_ = f32[32,128]{1,0:T(8,128)S(1)} collective-permute-done((f32[32,128]{1,0:T(8,128)S(1)}, f32[32,128]{1,0:T(8,128)S(1)}, u32[]{:S(2)}, u32[]{:S(2)}) %collective-permute-start.14) | collective-permute-done | bytes 16416 | tf_op jit(solution)/shard_map/ppermute | solution.py:38
  94.5 1.6 %collective-permute-start.17 = (bf16[32,896]{1,0:T(8,128)(2,1)S(1)}, bf16[32,896]{1,0:T(8,128)(2,1)S(1)}, u32[]{:S(2)}, u32[]{:S(2)}) collective-permute-start(bf16[32,896]{1,0:T(8,128)(2,1)S(1)} %finish.2), channel_id=1, source_target_pairs={{0,4},{1,5},{2,6},{3,7},{4,0},{5,1},{6,2},{7,3},{8,12},{9,13},{10,... | collective-permute-start | bytes 172040 | tf_op jit(solution)/shard_map/ppermute | solution.py:38
  96.1 3.5 %collective-permute-done.16 = bf16[32,896]{1,0:T(8,128)(2,1)S(1)} collective-permute-done((bf16[32,896]{1,0:T(8,128)(2,1)S(1)}, bf16[32,896]{1,0:T(8,128)(2,1)S(1)}, u32[]{:S(2)}, u32[]{:S(2)}) %collective-permute-start.16) | collective-permute-done | bytes 57376 | tf_op jit(solution)/shard_map/ppermute | solution.py:38
  99.7 0.6 collective-permute-done.17
  100.3 0.5 collective-permute-start.34
  100.8 0.4 collective-permute-start.38
  101.6 4.0 %collective-permute-done.18 = bf16[32,896]{1,0:T(8,128)(2,1)S(1)} collective-permute-done((bf16[32,896]{1,0:T(8,128)(2,1)S(1)}, bf16[32,896]{1,0:T(8,128)(2,1)S(1)}, u32[]{:S(2)}, u32[]{:S(2)}) %collective-permute-start.18) | collective-permute-done | bytes 57376 | tf_op jit(solution)/shard_map/ppermute | solution.py:38
  105.6 0.5 collective-permute-start.19
  106.2 1.0 collective-permute-start.20
  107.1 2.1 %collective-permute-start.21 = (bf16[128,896]{1,0:T(8,128)(2,1)S(1)}, bf16[128,896]{1,0:T(8,128)(2,1)S(1)}, u32[]{:S(2)}, u32[]{:S(2)}) collective-permute-start(bf16[128,896]{1,0:T(8,128)(2,1)S(1)} %pad_maximum_fusion.refs_0_), channel_id=1, source_target_pairs={{0,17},{1,16},{2,19},{3,18},{4,21},{5,20},{6,23},{7,22},{8,25},{9,... | collective-permute-start | bytes 688136 | tf_op jit(solution)/shard_map/ppermute | solution.py:48
  109.2 14.9 %vocab.2 = f32[8,256]{1,0:T(8,128)S(1)} custom-call(s32[40]{0:T(128)S(1)} %concatenate.17.at, s32[256,1]{1,0:T(8,128)S(1)} %copy.23.targets, bf16[128,896]{1,0:T(8,128)(2,1)S(1)} %pad_maximum_fusion.1.refs_0_, bf16[128,896]{1,0:T(8,128)(2,1)S(1)} %collective-permute-done.32.refs_1_, bf16[128,896]{1,0:T(8,128)(2,1)S(1)} %collective-permute-done.33.refs_2_, ...), custom_call_target="tpu_custom_call" | custom-call | flops 7516192768 | bytes 29360128 | tf_op jit(solution)/shard_map/vocab/pallas_call | solution.py:489
  124.2 0.5 collective-permute-start.40
  126.7 14.9 %vocab.3 = f32[8,256]{1,0:T(8,128)S(1)} custom-call(s32[40]{0:T(128)S(1)} %concatenate.17.at, s32[256,1]{1,0:T(8,128)S(1)} %copy.24.targets, bf16[128,896]{1,0:T(8,128)(2,1)S(1)} %pad_maximum_fusion.refs_0_, bf16[128,896]{1,0:T(8,128)(2,1)S(1)} %collective-permute-done.39.refs_1_, bf16[128,896]{1,0:T(8,128)(2,1)S(1)} %collective-permute-done.19.refs_2_, ...), custom_call_target="tpu_custom_call" | custom-call | flops 7516192768 | bytes 29360128 | tf_op jit(solution)/shard_map/vocab/pallas_call | solution.py:489
  141.6 0.7 broadcast_in_dim.63
  142.3 2.6 %all-to-all-start = ((f32[32,3,512]{2,1,0:T(4,128)}), f32[32,3,512]{2,1,0:T(4,128)S(1)}, u32[]{:S(2)}, u32[]{:S(2)}) async-start(f32[32,3,512]{2,1,0:T(4,128)} %broadcast_in_dim.63), calls=%async_computation | async-start | bytes 524288 | tf_op jit(solution)/shard_map/all_to_all | solution.py:655
  144.9 10.4 %all-to-all-done = f32[32,3,512]{2,1,0:T(4,128)S(1)} async-done(((f32[32,3,512]{2,1,0:T(4,128)}), f32[32,3,512]{2,1,0:T(4,128)S(1)}, u32[]{:S(2)}, u32[]{:S(2)}) %all-to-all-start) | async-done | bytes 196640 | tf_op jit(solution)/shard_map/all_to_all | solution.py:655
  155.4 0.5 fusion.4
  156.2 0.5 maximum_divide_fusion
  (107 shorter events, 5.1 us)
Async XLA Ops:
  0.6 5.2 %copy-start.11 = (f32[3584]{0:T(1024)S(1)}, f32[3584]{0:T(1024)}, u32[]{:S(2)}) copy-start(f32[3584]{0:T(1024)} %param.30) | copy-start | bytes 43012
  0.7 1.2 copy-start.7
  1.9 4.1 %copy-start.3 = (s32[2]{0:T(128)}, s32[2]{0:T(128)S(1)}, u32[]{:S(2)}) copy-start(s32[2]{0:T(128)S(1)} %pad_add_fusion.3.ids) | copy-start | bytes 28
  1.9 3.9 %copy-start.12 = (f32[3584]{0:T(1024)S(1)}, f32[3584]{0:T(1024)}, u32[]{:S(2)}) copy-start(f32[3584]{0:T(1024)} %param.31) | copy-start | bytes 43012
  1.9 3.9 %copy-start.13 = (f32[3584]{0:T(1024)S(1)}, f32[3584]{0:T(1024)}, u32[]{:S(2)}) copy-start(f32[3584]{0:T(1024)} %param.32) | copy-start | bytes 43012
  2.8 10.7 %collective-permute-start.2 = (bf16[136,896]{1,0:T(8,128)(2,1)S(1)}, bf16[136,896]{1,0:T(8,128)(2,1)S(1)}, u32[]{:S(2)}, u32[]{:S(2)}) collective-permute-start(bf16[136,896]{1,0:T(8,128)(2,1)S(1)} %get-tuple-element.35), channel_id=1, source_target_pairs={{0,16},{8,24},{16,0},{24,8},{1,17},{9,25},{17,1},{25,9},{2,18},{10... | collective-permute-start | bytes 731144 | tf_op jit(solution)/shard_map/ppermute | solution.py:38
  5.8 10.4 %collective-permute-start.3 = (bf16[136,896]{1,0:T(8,128)(2,1)S(1)}, bf16[136,896]{1,0:T(8,128)(2,1)S(1)}, u32[]{:S(2)}, u32[]{:S(2)}) collective-permute-start(bf16[136,896]{1,0:T(8,128)(2,1)S(1)} %get-tuple-element.36), channel_id=1, source_target_pairs={{0,24},{8,16},{16,8},{24,0},{1,25},{9,17},{17,9},{25,1},{2,26},{10... | collective-permute-start | bytes 731144 | tf_op jit(solution)/shard_map/ppermute | solution.py:38
  6.0 10.2 %copy-start.2 = (s32[4]{0:T(128)S(1)}, s32[4]{0:T(128)}, u32[]{:S(2)}) copy-start(s32[4]{0:T(128)} %cand_of.5) | copy-start | bytes 52
  6.0 10.2 %copy-start.5 = (f32[4]{0:T(128)S(1)}, f32[4]{0:T(128)}, u32[]{:S(2)}) copy-start(f32[4]{0:T(128)} %lambdas.5) | copy-start | bytes 52
  16.2 2.0 %copy-start = (bf16[896,2048]{1,0:T(8,128)(2,1)S(1)}, bf16[896,2048]{1,0:T(8,128)(2,1)}, u32[]{:S(2)}) copy-start(bf16[896,2048]{1,0:T(8,128)(2,1)} %prep.1.refs_3_) | copy-start | bytes 11010052
  18.2 0.7 copy-start.4
  18.9 4.6 %copy-start.1 = (bf16[896,2048]{1,0:T(8,128)(2,1)S(1)}, bf16[896,2048]{1,0:T(8,128)(2,1)}, u32[]{:S(2)}) copy-start(bf16[896,2048]{1,0:T(8,128)(2,1)} %prep.1.refs_3_) | copy-start | bytes 11010052
  21.0 5.1 %collective-permute-start.4 = (f32[128,1024]{1,0:T(8,128)S(1)}, f32[128,1024]{1,0:T(8,128)S(1)}, u32[]{:S(2)}, u32[]{:S(2)}) collective-permute-start(f32[128,1024]{1,0:T(8,128)S(1)} %get-tuple-element.38), channel_id=1, source_target_pairs={{0,8},{8,0},{16,24},{24,16},{1,9},{9,1},{17,25},{25,17},{2,10},{10... | collective-permute-start | bytes 1572872 | tf_op jit(solution)/shard_map/ppermute | solution.py:38
  21.6 1.9 %collective-permute-start = (bf16[136,896]{1,0:T(8,128)(2,1)S(1)}, bf16[136,896]{1,0:T(8,128)(2,1)S(1)}, u32[]{:S(2)}, u32[]{:S(2)}) collective-permute-start(bf16[136,896]{1,0:T(8,128)(2,1)S(1)} %get-tuple-element.32), channel_id=1, source_target_pairs={{0,8},{8,0},{16,24},{24,16},{1,9},{9,1},{17,25},{25,17},{2,10},{10... | collective-permute-start | bytes 731144 | tf_op jit(solution)/shard_map/ppermute | solution.py:38
  23.5 16.7 %copy-start.6 = (bf16[2,512,896]{2,1,0:T(8,128)(2,1)S(1)}, bf16[2,512,896]{2,1,0:T(8,128)(2,1)}, u32[]{:S(2)}) copy-start(bf16[2,512,896]{2,1,0:T(8,128)(2,1)} %delta.1) | copy-start | bytes 5505028
  25.6 2.6 %collective-permute-start.1 = (f32[128,1024]{1,0:T(8,128)S(1)}, f32[128,1024]{1,0:T(8,128)S(1)}, u32[]{:S(2)}, u32[]{:S(2)}) collective-permute-start(f32[128,1024]{1,0:T(8,128)S(1)} %get-tuple-element.34), channel_id=1, source_target_pairs={{0,8},{8,0},{16,24},{24,16},{1,9},{9,1},{17,25},{25,17},{2,10},{10... | collective-permute-start | bytes 1572872 | tf_op jit(solution)/shard_map/ppermute | solution.py:38
  26.1 8.4 %collective-permute-start.5 = (bf16[128,1024]{1,0:T(8,128)(2,1)S(1)}, bf16[128,1024]{1,0:T(8,128)(2,1)S(1)}, u32[]{:S(2)}, u32[]{:S(2)}) collective-permute-start(bf16[128,1024]{1,0:T(8,128)(2,1)S(1)} %join.1), channel_id=1, source_target_pairs={{0,16},{8,24},{16,0},{24,8},{1,17},{9,25},{17,1},{25,9},{2,18},{10... | collective-permute-start | bytes 786440 | tf_op jit(solution)/shard_map/ppermute | solution.py:38
  35.2 5.0 %collective-permute-start.7 = (bf16[128,512]{1,0:T(8,128)(2,1)S(1)}, bf16[128,512]{1,0:T(8,128)(2,1)S(1)}, u32[]{:S(2)}, u32[]{:S(2)}) collective-permute-start(bf16[128,512]{1,0:T(8,128)(2,1)S(1)} %attend.1.refs_0_), channel_id=1, source_target_pairs={{0,16},{8,24},{16,0},{24,8},{1,17},{9,25},{17,1},{25,9},{2,18},{10... | collective-permute-start | bytes 393224 | tf_op jit(solution)/shard_map/ppermute | solution.py:38
  37.1 4.7 %collective-permute-start.6 = (bf16[128,512]{1,0:T(8,128)(2,1)S(1)}, bf16[128,512]{1,0:T(8,128)(2,1)S(1)}, u32[]{:S(2)}, u32[]{:S(2)}) collective-permute-start(bf16[128,512]{1,0:T(8,128)(2,1)S(1)} %attend.1.refs_0_), channel_id=1, source_target_pairs={{0,8},{8,0},{16,24},{24,16},{1,9},{9,1},{17,25},{25,17},{2,10},{10... | collective-permute-start | bytes 393224 | tf_op jit(solution)/shard_map/ppermute | solution.py:38
  40.2 1.5 collective-permute-start.8
  40.7 1.0 copy-start.9
  41.7 1.2 copy-start.8
  42.9 1.2 copy-start.10
  47.0 8.1 %collective-permute-start.22 = (bf16[1,128,896]{2,1,0:T(8,128)(2,1)S(1)}, bf16[1,128,896]{2,1,0:T(8,128)(2,1)S(1)}, u32[]{:S(2)}, u32[]{:S(2)}) collective-permute-start(bf16[1,128,896]{2,1,0:T(8,128)(2,1)S(1)} %get-tuple-element.69), channel_id=1, source_target_pairs={{0,1},{1,0},{2,3},{3,2},{4,5},{5,4},{6,7},{7,6},{8,9},{9,8},{10,11... | collective-permute-start | bytes 688136 | tf_op jit(solution)/shard_map/ppermute | solution.py:38
  55.7 6.2 %collective-permute-start.23 = (bf16[32,896]{1,0:T(8,128)(2,1)S(1)}, bf16[32,896]{1,0:T(8,128)(2,1)S(1)}, u32[]{:S(2)}, u32[]{:S(2)}) collective-permute-start(bf16[32,896]{1,0:T(8,128)(2,1)S(1)} %get-tuple-element.49), channel_id=1, source_target_pairs={{0,2},{1,3},{2,0},{3,1},{4,6},{5,7},{6,4},{7,5},{8,10},{9,11},{10,... | collective-permute-start | bytes 172040 | tf_op jit(solution)/shard_map/ppermute | solution.py:38
  57.6 6.0 %collective-permute-start.24 = (bf16[32,896]{1,0:T(8,128)(2,1)S(1)}, bf16[32,896]{1,0:T(8,128)(2,1)S(1)}, u32[]{:S(2)}, u32[]{:S(2)}) collective-permute-start(bf16[32,896]{1,0:T(8,128)(2,1)S(1)} %get-tuple-element.50), channel_id=1, source_target_pairs={{0,4},{1,5},{2,6},{3,7},{4,0},{5,1},{6,2},{7,3},{8,12},{9,13},{10,... | collective-permute-start | bytes 172040 | tf_op jit(solution)/shard_map/ppermute | solution.py:38
  60.2 6.0 %collective-permute-start.25 = (bf16[32,896]{1,0:T(8,128)(2,1)S(1)}, bf16[32,896]{1,0:T(8,128)(2,1)S(1)}, u32[]{:S(2)}, u32[]{:S(2)}) collective-permute-start(bf16[32,896]{1,0:T(8,128)(2,1)S(1)} %get-tuple-element.51), channel_id=1, source_target_pairs={{0,6},{1,7},{2,4},{3,5},{4,2},{5,3},{6,0},{7,1},{8,14},{9,15},{10,... | collective-permute-start | bytes 172040 | tf_op jit(solution)/shard_map/ppermute | solution.py:38
  60.3 16.1 %collective-permute-start.9 = (bf16[1,128,896]{2,1,0:T(8,128)(2,1)S(1)}, bf16[1,128,896]{2,1,0:T(8,128)(2,1)S(1)}, u32[]{:S(2)}, u32[]{:S(2)}) collective-permute-start(bf16[1,128,896]{2,1,0:T(8,128)(2,1)S(1)} %get-tuple-element.70), channel_id=1, source_target_pairs={{0,1},{1,0},{2,3},{3,2},{4,5},{5,4},{6,7},{7,6},{8,9},{9,8},{10,11... | collective-permute-start | bytes 688136 | tf_op jit(solution)/shard_map/ppermute | solution.py:38
  66.9 2.0 %collective-permute-start.26 = (f32[32,128]{1,0:T(8,128)S(1)}, f32[32,128]{1,0:T(8,128)S(1)}, u32[]{:S(2)}, u32[]{:S(2)}) collective-permute-start(f32[32,128]{1,0:T(8,128)S(1)} %get-tuple-element.54.refs_0_), channel_id=1, source_target_pairs={{0,8},{8,0},{16,24},{24,16},{1,9},{9,1},{17,25},{25,17},{2,10},{10... | collective-permute-start | bytes 49160 | tf_op jit(solution)/shard_map/ppermute | solution.py:38
  67.0 3.8 %collective-permute-start.27 = (f32[32,128]{1,0:T(8,128)S(1)}, f32[32,128]{1,0:T(8,128)S(1)}, u32[]{:S(2)}, u32[]{:S(2)}) collective-permute-start(f32[32,128]{1,0:T(8,128)S(1)} %get-tuple-element.54.refs_0_), channel_id=1, source_target_pairs={{0,16},{8,24},{16,0},{24,8},{1,17},{9,25},{17,1},{25,9},{2,18},{10... | collective-permute-start | bytes 49160 | tf_op jit(solution)/shard_map/ppermute | solution.py:38
  68.5 3.2 %collective-permute-start.28 = (f32[32,128]{1,0:T(8,128)S(1)}, f32[32,128]{1,0:T(8,128)S(1)}, u32[]{:S(2)}, u32[]{:S(2)}) collective-permute-start(f32[32,128]{1,0:T(8,128)S(1)} %get-tuple-element.54.refs_0_), channel_id=1, source_target_pairs={{0,24},{8,16},{16,8},{24,0},{1,25},{9,17},{17,9},{25,1},{2,26},{10... | collective-permute-start | bytes 49160 | tf_op jit(solution)/shard_map/ppermute | solution.py:38
  71.9 6.8 %collective-permute-start.29 = (bf16[32,896]{1,0:T(8,128)(2,1)S(1)}, bf16[32,896]{1,0:T(8,128)(2,1)S(1)}, u32[]{:S(2)}, u32[]{:S(2)}) collective-permute-start(bf16[32,896]{1,0:T(8,128)(2,1)S(1)} %finish.3), channel_id=1, source_target_pairs={{0,2},{1,3},{2,0},{3,1},{4,6},{5,7},{6,4},{7,5},{8,10},{9,11},{10,... | collective-permute-start | bytes 172040 | tf_op jit(solution)/shard_map/ppermute | solution.py:38
  72.0 9.4 %collective-permute-start.30 = (bf16[32,896]{1,0:T(8,128)(2,1)S(1)}, bf16[32,896]{1,0:T(8,128)(2,1)S(1)}, u32[]{:S(2)}, u32[]{:S(2)}) collective-permute-start(bf16[32,896]{1,0:T(8,128)(2,1)S(1)} %finish.3), channel_id=1, source_target_pairs={{0,4},{1,5},{2,6},{3,7},{4,0},{5,1},{6,2},{7,3},{8,12},{9,13},{10,... | collective-permute-start | bytes 172040 | tf_op jit(solution)/shard_map/ppermute | solution.py:38
  73.7 7.8 %collective-permute-start.31 = (bf16[32,896]{1,0:T(8,128)(2,1)S(1)}, bf16[32,896]{1,0:T(8,128)(2,1)S(1)}, u32[]{:S(2)}, u32[]{:S(2)}) collective-permute-start(bf16[32,896]{1,0:T(8,128)(2,1)S(1)} %finish.3), channel_id=1, source_target_pairs={{0,6},{1,7},{2,4},{3,5},{4,2},{5,3},{6,0},{7,1},{8,14},{9,15},{10,... | collective-permute-start | bytes 172040 | tf_op jit(solution)/shard_map/ppermute | solution.py:38
  77.0 6.7 %collective-permute-start.10 = (bf16[32,896]{1,0:T(8,128)(2,1)S(1)}, bf16[32,896]{1,0:T(8,128)(2,1)S(1)}, u32[]{:S(2)}, u32[]{:S(2)}) collective-permute-start(bf16[32,896]{1,0:T(8,128)(2,1)S(1)} %get-tuple-element.42), channel_id=1, source_target_pairs={{0,2},{1,3},{2,0},{3,1},{4,6},{5,7},{6,4},{7,5},{8,10},{9,11},{10,... | collective-permute-start | bytes 172040 | tf_op jit(solution)/shard_map/ppermute | solution.py:38
  77.1 8.0 %collective-permute-start.11 = (bf16[32,896]{1,0:T(8,128)(2,1)S(1)}, bf16[32,896]{1,0:T(8,128)(2,1)S(1)}, u32[]{:S(2)}, u32[]{:S(2)}) collective-permute-start(bf16[32,896]{1,0:T(8,128)(2,1)S(1)} %get-tuple-element.43), channel_id=1, source_target_pairs={{0,4},{1,5},{2,6},{3,7},{4,0},{5,1},{6,2},{7,3},{8,12},{9,13},{10,... | collective-permute-start | bytes 172040 | tf_op jit(solution)/shard_map/ppermute | solution.py:38
  78.7 6.3 %collective-permute-start.12 = (bf16[32,896]{1,0:T(8,128)(2,1)S(1)}, bf16[32,896]{1,0:T(8,128)(2,1)S(1)}, u32[]{:S(2)}, u32[]{:S(2)}) collective-permute-start(bf16[32,896]{1,0:T(8,128)(2,1)S(1)} %get-tuple-element.44), channel_id=1, source_target_pairs={{0,6},{1,7},{2,4},{3,5},{4,2},{5,3},{6,0},{7,1},{8,14},{9,15},{10,... | collective-permute-start | bytes 172040 | tf_op jit(solution)/shard_map/ppermute | solution.py:38
  81.5 18.8 %collective-permute-start.33 = (bf16[128,896]{1,0:T(8,128)(2,1)S(1)}, bf16[128,896]{1,0:T(8,128)(2,1)S(1)}, u32[]{:S(2)}, u32[]{:S(2)}) collective-permute-start(bf16[128,896]{1,0:T(8,128)(2,1)S(1)} %pad_maximum_fusion.1.refs_0_), channel_id=1, source_target_pairs={{0,1},{1,0},{2,3},{3,2},{4,5},{5,4},{6,7},{7,6},{8,9},{9,8},{10,11... | collective-permute-start | bytes 688136 | tf_op jit(solution)/shard_map/ppermute | solution.py:48
  83.0 17.7 %collective-permute-start.35 = (bf16[128,896]{1,0:T(8,128)(2,1)S(1)}, bf16[128,896]{1,0:T(8,128)(2,1)S(1)}, u32[]{:S(2)}, u32[]{:S(2)}) collective-permute-start(bf16[128,896]{1,0:T(8,128)(2,1)S(1)} %pad_maximum_fusion.1.refs_0_), channel_id=1, source_target_pairs={{0,16},{1,17},{2,18},{3,19},{4,20},{5,21},{6,22},{7,23},{8,24},{9,... | collective-permute-start | bytes 688136 | tf_op jit(solution)/shard_map/ppermute | solution.py:48
  83.7 17.1 %collective-permute-start.37 = (bf16[128,896]{1,0:T(8,128)(2,1)S(1)}, bf16[128,896]{1,0:T(8,128)(2,1)S(1)}, u32[]{:S(2)}, u32[]{:S(2)}) collective-permute-start(bf16[128,896]{1,0:T(8,128)(2,1)S(1)} %pad_maximum_fusion.1.refs_0_), channel_id=1, source_target_pairs={{0,17},{1,16},{2,19},{3,18},{4,21},{5,20},{6,23},{7,22},{8,25},{9,... | collective-permute-start | bytes 688136 | tf_op jit(solution)/shard_map/ppermute | solution.py:48
  85.1 16.2 %copy-start.14 = (s32[512]{0:T(512)S(1)}, s32[512]{0:T(512)}, u32[]{:S(2)}) copy-start(s32[512]{0:T(512)} %param.18) | copy-start | bytes 6148
  86.0 1.2 collective-permute-start.13
  86.1 8.1 %collective-permute-start.14 = (f32[32,128]{1,0:T(8,128)S(1)}, f32[32,128]{1,0:T(8,128)S(1)}, u32[]{:S(2)}, u32[]{:S(2)}) collective-permute-start(f32[32,128]{1,0:T(8,128)S(1)} %get-tuple-element.47.refs_0_), channel_id=1, source_target_pairs={{0,16},{8,24},{16,0},{24,8},{1,17},{9,25},{17,1},{25,9},{2,18},{10... | collective-permute-start | bytes 49160 | tf_op jit(solution)/shard_map/ppermute | solution.py:38
  87.2 6.9 %collective-permute-start.15 = (f32[32,128]{1,0:T(8,128)S(1)}, f32[32,128]{1,0:T(8,128)S(1)}, u32[]{:S(2)}, u32[]{:S(2)}) collective-permute-start(f32[32,128]{1,0:T(8,128)S(1)} %get-tuple-element.47.refs_0_), channel_id=1, source_target_pairs={{0,24},{8,16},{16,8},{24,0},{1,25},{9,17},{17,9},{25,1},{2,26},{10... | collective-permute-start | bytes 49160 | tf_op jit(solution)/shard_map/ppermute | solution.py:38
  94.4 5.2 %collective-permute-start.16 = (bf16[32,896]{1,0:T(8,128)(2,1)S(1)}, bf16[32,896]{1,0:T(8,128)(2,1)S(1)}, u32[]{:S(2)}, u32[]{:S(2)}) collective-permute-start(bf16[32,896]{1,0:T(8,128)(2,1)S(1)} %finish.2), channel_id=1, source_target_pairs={{0,2},{1,3},{2,0},{3,1},{4,6},{5,7},{6,4},{7,5},{8,10},{9,11},{10,... | collective-permute-start | bytes 172040 | tf_op jit(solution)/shard_map/ppermute | solution.py:38
  94.5 5.8 %collective-permute-start.17 = (bf16[32,896]{1,0:T(8,128)(2,1)S(1)}, bf16[32,896]{1,0:T(8,128)(2,1)S(1)}, u32[]{:S(2)}, u32[]{:S(2)}) collective-permute-start(bf16[32,896]{1,0:T(8,128)(2,1)S(1)} %finish.2), channel_id=1, source_target_pairs={{0,4},{1,5},{2,6},{3,7},{4,0},{5,1},{6,2},{7,3},{8,12},{9,13},{10,... | collective-permute-start | bytes 172040 | tf_op jit(solution)/shard_map/ppermute | solution.py:38
  99.6 6.0 %collective-permute-start.18 = (bf16[32,896]{1,0:T(8,128)(2,1)S(1)}, bf16[32,896]{1,0:T(8,128)(2,1)S(1)}, u32[]{:S(2)}, u32[]{:S(2)}) collective-permute-start(bf16[32,896]{1,0:T(8,128)(2,1)S(1)} %finish.2), channel_id=1, source_target_pairs={{0,6},{1,7},{2,4},{3,5},{4,2},{5,3},{6,0},{7,1},{8,14},{9,15},{10,... | collective-permute-start | bytes 172040 | tf_op jit(solution)/shard_map/ppermute | solution.py:38
  100.3 5.9 %collective-permute-start.32 = (bf16[128,896]{1,0:T(8,128)(2,1)S(1)}, bf16[128,896]{1,0:T(8,128)(2,1)S(1)}, u32[]{:S(2)}, u32[]{:S(2)}) collective-permute-start(bf16[128,896]{1,0:T(8,128)(2,1)S(1)} %pad_maximum_fusion.1.refs_0_), channel_id=1, source_target_pairs={{0,8},{8,0},{16,24},{24,16},{1,9},{9,1},{17,25},{25,17},{2,10},{10... | collective-permute-start | bytes 688136 | tf_op jit(solution)/shard_map/ppermute | solution.py:38
  100.3 6.9 %collective-permute-start.34 = (bf16[128,896]{1,0:T(8,128)(2,1)S(1)}, bf16[128,896]{1,0:T(8,128)(2,1)S(1)}, u32[]{:S(2)}, u32[]{:S(2)}) collective-permute-start(bf16[128,896]{1,0:T(8,128)(2,1)S(1)} %collective-permute-done.33.refs_2_), channel_id=1, source_target_pairs={{0,8},{8,0},{16,24},{24,16},{1,9},{9,1},{17,25},{25,17},{2,10},{10... | collective-permute-start | bytes 688136 | tf_op jit(solution)/shard_map/ppermute | solution.py:38
  100.8 8.4 %collective-permute-start.36 = (bf16[128,896]{1,0:T(8,128)(2,1)S(1)}, bf16[128,896]{1,0:T(8,128)(2,1)S(1)}, u32[]{:S(2)}, u32[]{:S(2)}) collective-permute-start(bf16[128,896]{1,0:T(8,128)(2,1)S(1)} %collective-permute-done.35.refs_4_), channel_id=1, source_target_pairs={{0,8},{8,0},{16,24},{24,16},{1,9},{9,1},{17,25},{25,17},{2,10},{10... | collective-permute-start | bytes 688136 | tf_op jit(solution)/shard_map/ppermute | solution.py:38
  100.8 8.4 %collective-permute-start.38 = (bf16[128,896]{1,0:T(8,128)(2,1)S(1)}, bf16[128,896]{1,0:T(8,128)(2,1)S(1)}, u32[]{:S(2)}, u32[]{:S(2)}) collective-permute-start(bf16[128,896]{1,0:T(8,128)(2,1)S(1)} %collective-permute-done.37.refs_6_), channel_id=1, source_target_pairs={{0,8},{8,0},{16,24},{24,16},{1,9},{9,1},{17,25},{25,17},{2,10},{10... | collective-permute-start | bytes 688136 | tf_op jit(solution)/shard_map/ppermute | solution.py:38
  105.6 19.8 %copy-start.15 = (s32[128]{0:T(128)S(1)}, s32[128]{0:T(128)}, u32[]{:S(2)}) copy-start(s32[128]{0:T(128)} %param.19) | copy-start | bytes 1540
  105.6 18.5 %collective-permute-start.19 = (bf16[128,896]{1,0:T(8,128)(2,1)S(1)}, bf16[128,896]{1,0:T(8,128)(2,1)S(1)}, u32[]{:S(2)}, u32[]{:S(2)}) collective-permute-start(bf16[128,896]{1,0:T(8,128)(2,1)S(1)} %pad_maximum_fusion.refs_0_), channel_id=1, source_target_pairs={{0,1},{1,0},{2,3},{3,2},{4,5},{5,4},{6,7},{7,6},{8,9},{9,8},{10,11... | collective-permute-start | bytes 688136 | tf_op jit(solution)/shard_map/ppermute | solution.py:48
  106.2 18.0 %collective-permute-start.20 = (bf16[128,896]{1,0:T(8,128)(2,1)S(1)}, bf16[128,896]{1,0:T(8,128)(2,1)S(1)}, u32[]{:S(2)}, u32[]{:S(2)}) collective-permute-start(bf16[128,896]{1,0:T(8,128)(2,1)S(1)} %pad_maximum_fusion.refs_0_), channel_id=1, source_target_pairs={{0,16},{1,17},{2,18},{3,19},{4,20},{5,21},{6,22},{7,23},{8,24},{9,... | collective-permute-start | bytes 688136 | tf_op jit(solution)/shard_map/ppermute | solution.py:48
  107.1 17.0 %collective-permute-start.21 = (bf16[128,896]{1,0:T(8,128)(2,1)S(1)}, bf16[128,896]{1,0:T(8,128)(2,1)S(1)}, u32[]{:S(2)}, u32[]{:S(2)}) collective-permute-start(bf16[128,896]{1,0:T(8,128)(2,1)S(1)} %pad_maximum_fusion.refs_0_), channel_id=1, source_target_pairs={{0,17},{1,16},{2,19},{3,18},{4,21},{5,20},{6,23},{7,22},{8,25},{9,... | collective-permute-start | bytes 688136 | tf_op jit(solution)/shard_map/ppermute | solution.py:48
  124.1 1.6 collective-permute-start.39
  124.2 1.8 %collective-permute-start.40 = (bf16[128,896]{1,0:T(8,128)(2,1)S(1)}, bf16[128,896]{1,0:T(8,128)(2,1)S(1)}, u32[]{:S(2)}, u32[]{:S(2)}) collective-permute-start(bf16[128,896]{1,0:T(8,128)(2,1)S(1)} %collective-permute-done.19.refs_2_), channel_id=1, source_target_pairs={{0,8},{8,0},{16,24},{24,16},{1,9},{9,1},{17,25},{25,17},{2,10},{10... | collective-permute-start | bytes 688136 | tf_op jit(solution)/shard_map/ppermute | solution.py:38
  124.7 1.6 %collective-permute-start.41 = (bf16[128,896]{1,0:T(8,128)(2,1)S(1)}, bf16[128,896]{1,0:T(8,128)(2,1)S(1)}, u32[]{:S(2)}, u32[]{:S(2)}) collective-permute-start(bf16[128,896]{1,0:T(8,128)(2,1)S(1)} %collective-permute-done.20.refs_4_), channel_id=1, source_target_pairs={{0,8},{8,0},{16,24},{24,16},{1,9},{9,1},{17,25},{25,17},{2,10},{10... | collective-permute-start | bytes 688136 | tf_op jit(solution)/shard_map/ppermute | solution.py:38
  124.8 1.9 %collective-permute-start.42 = (bf16[128,896]{1,0:T(8,128)(2,1)S(1)}, bf16[128,896]{1,0:T(8,128)(2,1)S(1)}, u32[]{:S(2)}, u32[]{:S(2)}) collective-permute-start(bf16[128,896]{1,0:T(8,128)(2,1)S(1)} %collective-permute-done.21.refs_6_), channel_id=1, source_target_pairs={{0,8},{8,0},{16,24},{24,16},{1,9},{9,1},{17,25},{25,17},{2,10},{10... | collective-permute-start | bytes 688136 | tf_op jit(solution)/shard_map/ppermute | solution.py:38
  142.3 13.0 %all-to-all-start = ((f32[32,3,512]{2,1,0:T(4,128)}), f32[32,3,512]{2,1,0:T(4,128)S(1)}, u32[]{:S(2)}, u32[]{:S(2)}) async-start(f32[32,3,512]{2,1,0:T(4,128)} %broadcast_in_dim.63), calls=%async_computation | async-start | bytes 524288 | tf_op jit(solution)/shard_map/all_to_all | solution.py:655

commit v2 on v1

--- a/solution.py
+++ b/solution.py
@@ -7,6 +7,7 @@
 from jax.experimental import pallas as pl
 from jax.experimental.pallas import tpu as pltpu
 from jax.sharding import PartitionSpec as P
+
 
 KV = 8
 HEAD_SIZE = 256
@@ -19,6 +20,7 @@
 
 VM = pl.BlockSpec(memory_space=pltpu.VMEM)
 SM = pl.BlockSpec(memory_space=pltpu.SMEM)
+FAR = pl.BlockSpec(memory_space=pl.ANY)
 
 
 def params(mib):
@@ -118,46 +120,58 @@
 
 
 def prep_body(ids, *refs):
-    *ins, out = refs
-    half = out.shape[1] // 2
+    *ins, delta_o, out, out_o = refs
+    delta_q, *ins = ins
     col = 0
-    for base, delta in zip(ins[::2], ins[1::2]):
-        width = base.shape[1]
-        out[:, col : col + width] = base[...]
-        out[:, half + col : half + col + width] = task_sum(delta)
-        col += width
-
-
-def prep_call(ids, pairs):
+    for base in ins[::2]:
+        out[:, col : col + base.shape[1]] = base[...]
+        col += base.shape[1]
+    for delta in [delta_q, *ins[1::2]]:
+        out[:, col : col + delta.shape[2]] = task_sum(delta)
+        col += delta.shape[2]
+    out_o[...] = task_sum(delta_o)
+
+
+def prep_call(ids, delta_q, pairs, delta_o):
     rows = pairs[0][0].shape[0]
-    tile = tile_of(rows, 128, 112, 64, 32, 16)
-    specs, operands, total_width = [], [], 0
-    for base, delta, width, of_head in pairs:
-        at = (lambda ids: ids[1]) if of_head else (lambda ids: 0)
-        specs.append(pl.BlockSpec((tile, width), lambda i, ids, at=at: (i, at(ids))))
-        specs.append(
-            pl.BlockSpec((delta.shape[0], tile, width), lambda i, ids, at=at: (0, i, at(ids)))
-        )
+    width_q = delta_q.shape[2]
+    tasks, rows_o, width_o = delta_o.shape
+    steps = 1
+    for choice in (2, 4, 8):
+        if rows % (16 * choice) == 0 and rows_o % (16 * choice) == 0:
+            steps = choice
+    tile, tile_o = rows // steps, rows_o // steps
+    specs = [pl.BlockSpec((tasks, tile, width_q), lambda i, ids: (0, i, 0))]
+    operands, total_width = [delta_q], width_q
+    for base, delta in pairs:
+        specs.append(pl.BlockSpec((tile, HEAD_SIZE), lambda i, ids: (i, ids[1])))
+        specs.append(pl.BlockSpec((tasks, tile, HEAD_SIZE), lambda i, ids: (0, i, ids[1])))
         operands += [base, delta]
-        total_width += width
+        total_width += 2 * HEAD_SIZE
+    specs.append(pl.BlockSpec((tasks, tile_o, width_o), lambda i, ids: (0, i, 0)))
     return pl.pallas_call(
         prep_body,
         grid_spec=pltpu.PrefetchScalarGridSpec(
             num_scalar_prefetch=1,
-            grid=(rows // tile,),
+            grid=(steps,),
             in_specs=specs,
-            out_specs=pl.BlockSpec((tile, 2 * total_width), lambda i, ids: (i, 0)),
+            out_specs=[
+                pl.BlockSpec((tile, total_width), lambda i, ids: (i, 0)),
+                pl.BlockSpec((tile_o, width_o), lambda i, ids: (i, 0)),
+            ],
         ),
-        out_shape=shape((rows, 2 * total_width), BF16),
+        out_shape=[shape((rows, total_width), BF16), shape((rows_o, width_o), BF16)],
         compiler_params=params(58),
         cost_estimate=cost(2e9, rows * total_width * 10),
         name="prep",
-    )(ids, *operands)
+    )(ids, *operands, delta_o)
 
 
 def qkv_body(count, first, ids, cand_of, lambdas, *refs):
-    pieces, gain, weights = refs[:count], refs[count], refs[count + 1]
-    outs, normed = refs[count + 2 : -1], refs[-1]
+    pieces, gain, base_q, weights = refs[:count], refs[count], refs[count + 1], refs[count + 2]
+    outs, normed = refs[-1 - count : -1], refs[-1]
+    width_q = base_q.shape[1]
+    rest = outs[0].shape[1] - width_q
     length, columns = outs[0].shape
     for k in range(count):
         turned = jnp.transpose(pieces[k][length:, :length].astype(F32))
@@ -166,12 +180,14 @@
         normed[k * length : (k + 1) * length, :] = (raw * column * gain[...][:1]).astype(BF16)
     chunk = tile_of(columns, 256, 128)
     for start in range(0, columns, chunk):
-        base = jnp.dot(
-            normed[...], weights[:, start : start + chunk], preferred_element_type=F32
-        )
+        if start < width_q:
+            first_term = base_q[:, start : start + chunk]
+        else:
+            first_term = weights[:, start - width_q : start - width_q + chunk]
+        base = jnp.dot(normed[...], first_term, preferred_element_type=F32)
         task = jnp.dot(
             normed[...],
-            weights[:, columns + start : columns + start + chunk],
+            weights[:, rest + start : rest + start + chunk],
             preferred_element_type=F32,
         )
         for k in range(count):
@@ -180,32 +196,32 @@
             outs[k][:, start : start + chunk] = base[rows] + mixing * task[rows]
 
 
-def qkv_call(ids, cand_of, lambdas, pieces, gain, weights, first):
+def qkv_call(ids, cand_of, lambdas, pieces, gain, base_q, weights, first, after):
     count = len(pieces)
     length, width = pieces[0].shape[0] - TAIL, pieces[0].shape[1]
-    columns = weights.shape[1] // 2
+    columns = (weights.shape[1] + base_q.shape[1]) // 2
     return pl.pallas_call(
         functools.partial(qkv_body, count, first),
-        in_specs=[SM] * 3 + [VM] * (count + 2),
+        in_specs=[SM] * 3 + [VM] * (count + 3) + [FAR] * len(after),
         out_specs=[VM] * count,
         out_shape=[shape((length, columns), F32)] * count,
         scratch_shapes=[pltpu.VMEM((count * length, width), BF16)],
         compiler_params=params(16),
         cost_estimate=cost(4 * count * length * width * columns, 2 * weights.size),
         name="qkv",
-    )(ids, cand_of, lambdas, *pieces, gain, weights)
+    )(ids, cand_of, lambdas, *pieces, gain, base_q, weights, *after)
 
 
 def join_body(own, other, out):
-    out[...] = (own[...] + other[...]).astype(BF16)
-
-
-def join_call(own, other):
+    out[...] = (own[...] + other[...]).astype(out.dtype)
+
+
+def join_call(own, other, dtype):
     return pl.pallas_call(
         join_body,
         in_specs=[VM, VM],
         out_specs=VM,
-        out_shape=shape(own.shape, BF16),
+        out_shape=shape(own.shape, dtype),
         compiler_params=params(4),
         cost_estimate=cost(1e8, 10 * own.size),
         name="join",
@@ -261,13 +277,21 @@
 
 
 def project_body(cands, group, ids, cand_of, lambdas, *refs):
-    contexts, base, task = refs[:cands], refs[cands], refs[cands + 1]
-    keep, send, stack = refs[cands + 2 :]
+    contexts, base_far, task_far = refs[:cands], refs[cands], refs[cands + 1]
+    keep, send, stack, base, task, sem = refs[cands + 2 :]
+    loads = [
+        pltpu.make_async_copy(base_far, base, sem.at[0]),
+        pltpu.make_async_copy(task_far, task, sem.at[1]),
+    ]
+    for load in loads:
+        load.start()
     own, bit = ids[0], ids[1]
     half = group // 2
     length, width = keep.shape[1:]
     for k in range(cands):
         stack[k * length : (k + 1) * length, :] = contexts[k][...]
+    for load in loads:
+        load.wait()
     for start in range(0, width, 256):
         cols = slice(start, min(start + 256, width))
         of_base = jnp.dot(stack[...], base[:, cols], preferred_element_type=F32)
@@ -296,33 +320,19 @@
     width = base.shape[1]
     return pl.pallas_call(
         functools.partial(project_body, cands, group),
-        in_specs=[SM] * 3 + [VM] * (cands + 2),
+        in_specs=[SM] * 3 + [VM] * cands + [FAR] * 2,
         out_specs=[VM, VM],
         out_shape=[shape((cands // 2, length, width), F32), shape((cands // 2, length, width), BF16)],
-        scratch_shapes=[pltpu.VMEM((cands * length, depth), BF16)],
+        scratch_shapes=[
+            pltpu.VMEM((cands * length, depth), BF16),
+            pltpu.VMEM(base.shape, BF16),
+            pltpu.VMEM(task.shape, BF16),
+            pltpu.SemaphoreType.DMA((2,)),
+        ],
         compiler_params=params(24),
         cost_estimate=cost(4 * cands * length * width * depth, 4 * base.size),
         name="project",
     )(ids, cand_of, lambdas, *contexts, base, task)
-
-
-def tasks_body(delta, out):
-    out[...] = task_sum(delta)
-
-
-def tasks_call(delta):
-    tasks, rows, width = delta.shape
-    tile = tile_of(rows, 128)
-    return pl.pallas_call(
-        tasks_body,
-        grid=(rows // tile,),
-        in_specs=[pl.BlockSpec((tasks, tile, width), lambda i: (0, i, 0))],
-        out_specs=pl.BlockSpec((tile, width), lambda i: (i, 0)),
-        out_shape=shape((rows, width), BF16),
-        compiler_params=params(16),
-        cost_estimate=cost(1e9, 6 * rows * width),
-        name="tasks",
-    )(delta)
 
 
 def spread_body(blocks, rows, ids, keep, got, own, *sends):
@@ -559,34 +569,31 @@
     for k in [*range(2, cands), 1]:
         xs[k] = swap(cuts[k], "cand", k)
 
-    weights = prep_call(
-        ids,
-        [
-            (base_q, delta_q, base_q.shape[1], False),
-            (base_k, delta_k, HEAD_SIZE, True),
-            (base_v, delta_v, HEAD_SIZE, True),
-        ],
+    weights, task_o = prep_call(
+        ids, delta_q, [(base_k, delta_k), (base_v, delta_v)], delta_o
     )
-    task_o = tasks_call(delta_o)
 
     gains = jnp.stack([pre_gain, post_gain, final_gain])
     gains = lax.dynamic_slice_in_dim(gains, own * width, width, 1)
     gain, post, final = (jnp.broadcast_to(gains[i : i + 1], (8, width)) for i in range(3))
     partials = []
+    after = []
     for first in range(0, cands, 2):
-        partials += qkv_call(
-            ids, cand_of, lambdas, xs[first : first + 2], gain, weights, first
-        )
+        inputs = xs[first : first + 2]
+        if first:
+            after = partials[-1:]
+        partials += qkv_call(ids, cand_of, lambdas, inputs, gain, base_q, weights, first, after)
     crossed = [swap(partials[k + 1], "cand", 1) for k in range(0, cands, 2)]
-    more = [crossed[0]]
+    more = []
     for k in range(2, cands, 2):
-        more.append(swap(join_call(partials[k], crossed[k // 2]), "cand", k))
+        more.append(swap(join_call(partials[k], crossed[k // 2], BF16), "cand", k))
 
     positions = jnp.arange(length).astype(F32)
     half = HEAD_SIZE // 2
     frequency = jnp.exp(-math.log(10000.0) * jnp.arange(half).astype(F32) * 2.0 / HEAD_SIZE)
     angles = positions[:, None] * frequency[None, :]
-    context = attend_call(partials[0], more, jnp.cos(angles), jnp.sin(angles), heads)
+    near = join_call(partials[0], crossed[0], F32)
+    context = attend_call(near, more, jnp.cos(angles), jnp.sin(angles), heads)
 
     contexts = [None] * cands
     contexts[0] = context
@@ -621,18 +628,20 @@
         crossing = []
         for cand_mask in range(0, cands, 2):
             for bit_mask in range(2):
-                moved = cand_mask or bit_mask
-                crossing.append(swap_both(pile, cand_mask, bit_mask) if moved else pile)
+                if cand_mask or bit_mask:
+                    crossing.append(swap_both(pile, cand_mask, bit_mask))
+                else:
+                    crossing.append(pile)
         arrived.append(crossing)
     for part in range(PARTS):
         crossing = arrived[part]
-        if part > 0:
-            crossing, results[-1] = lax.optimization_barrier((crossing, results[-1]))
         pieces, places = [], []
         for index, piece in enumerate(crossing):
             cand_mask, bit_mask = index // 2 * 2, index % 2
             for core_mask in range(2):
-                pieces.append(swap(piece, "cand", 1) if core_mask else piece)
+                if core_mask:
+                    piece = swap(piece, "cand", 1)
+                pieces.append(piece)
                 places.append(
                     jnp.stack(
                         [own ^ cand_mask ^ core_mask]
@@ -641,9 +650,7 @@
                 )
         vocab_start = (own * tensors + place) * unembed.shape[1]
         ids_here = targets[part * part_rows : (part + 1) * part_rows] - vocab_start
-        results.append(
-            vocab_call(pieces, places, ids_here.reshape(part_rows, 1), unembed, blocks)
-        )
+        results.append(vocab_call(pieces, places, ids_here.reshape(part_rows, 1), unembed, blocks))
     both = jnp.concatenate(results, axis=1)[:2]
     masks = jnp.where(
         (lax.broadcasted_iota(jnp.int32, (cands, 1), 0) == own) & (place == 0),
@@ -683,6 +690,5 @@
         P(None, ("cand", "tensor")),
     )
     out_specs = (P("cand"), P())
-    return jax.shard_map(
-        on_device, mesh=mesh, in_specs=in_specs, out_specs=out_specs, check_vma=False
-    )
+
+    return jax.shard_map(on_device, mesh=mesh, in_specs=in_specs, out_specs=out_specs, check_vma=False)

time: 157 us -> 148 us (0.943)
  waiting for transfers between devices: 53.8 us -> 45.9 us
  local copies, waits for them, and re-layouts: 8.54 us -> 4.98 us
    ppermute x37, waiting for transfers between devices: 43.3 us -> 22.3 us  [swap(): return lax.ppermute(value, axis, [(i, i ^ mask) for i in range(size)])]
    ppermute x6, waiting for transfers between devices: 0.02 us -> 13.1 us  [swap_both(): return lax.ppermute(value, ('cand', 'tensor'), pairs)]
    unnamed x32 -> x30, local copies, waits for them, and re-layouts: 7.23 us -> 3.67 us
  transfers between devices with their start and end apart: 44 -> 44, of which waited for: 19 -> 14; matrix products, arithmetic and copies ran while one was open for 1% -> 1% of each run, Pallas kernels for 18% -> 19%
where the time goes in v2:
time: 148 us; the launch traced here: 147 us
  Pallas kernels  50 us (34%)
  waiting for transfers between devices  45.9 us (31%)
  starting transfers between devices  42.9 us (29%)
  local copies, waits for them, and re-layouts  4.98 us (3%)
  other arithmetic  2.28 us (2%)
    ppermute x37, starting transfers between devices, swap(): return lax.ppermute(value, axis, [(i, i ^ mask) for i in range(size)])  32.6 us
    pallas_call x2, Pallas kernels, vocab_call(): pl.pallas_call(functools.partial(vocab_body, len(pieces), blocks, rows, w...  29.8 us
    ppermute x37, waiting for transfers between devices, swap(): return lax.ppermute(value, axis, [(i, i ^ mask) for i in range(size)])  22.3 us
    ppermute x6, waiting for transfers between devices, swap_both(): return lax.ppermute(value, ('cand', 'tensor'), pairs)  13.1 us
    all_to_all x1, waiting for transfers between devices, on_device(): summed = jnp.sum(lax.all_to_all(payload, ('cand', 'tensor'), 0, 0), axis=0)  10.4 us
    pallas_call x1, Pallas kernels, prep_call(): pl.pallas_call(prep_body, grid_spec=pltpu.PrefetchScalarGridSpec(num_scal...  7.94 us
    ppermute x6, starting transfers between devices, swap_both(): return lax.ppermute(value, ('cand', 'tensor'), pairs)  7.56 us
    pallas_call x2, Pallas kernels, qkv_call(): pl.pallas_call(functools.partial(qkv_body, count, first), in_specs=[SM] *...  4.13 us
  transfers between devices with their start and end apart: 44, of which 14 were waited for; matrix products, arithmetic and copies ran while one was open for 1% of the time, Pallas kernels for 19%

profile of v2, /device:TPU:0, one launch (start us, length us, event | category | flops | bytes accessed | tf_op | source)
XLA Modules:
  0.0 147.2 jit_solution(9679509248519640762)
XLA Ops:
  0.7 1.2 copy-done.7
  1.9 0.9 cut.1
  2.8 0.5 collective-permute-start
  3.3 2.6 %collective-permute-start.2 = (bf16[136,896]{1,0:T(8,128)(2,1)S(1)}, bf16[136,896]{1,0:T(8,128)(2,1)S(1)}, u32[]{:S(2)}, u32[]{:S(2)}) collective-permute-start(bf16[136,896]{1,0:T(8,128)(2,1)S(1)} %get-tuple-element.33), channel_id=1, source_target_pairs={{0,16},{8,24},{16,0},{24,8},{1,17},{9,25},{17,1},{25,9},{2,18},{10... | collective-permute-start | bytes 731144 | tf_op jit(solution)/shard_map/ppermute | solution.py:40
  6.2 7.9 %prep.1 = (bf16[896,1536]{1,0:T(8,128)(2,1)}, bf16[512,896]{1,0:T(8,128)(2,1)}) custom-call(s32[2]{0:T(128)} %copy-done.3, bf16[2,896,512]{2,1,0:T(8,128)(2,1)} %refs_0_.1, bf16[896,2048]{1,0:T(8,128)(2,1)} %refs_1_.1, bf16[2,896,2048]{2,1,0:T(8,128)(2,1)} %refs_2_.1, bf16[896,2048]{1,0:T(8,128)(2,1)} %refs_3_.3, bf16[2,896,2048]{2,1,0:T(8,128)(2,1)} %refs_4_.2, ...), custom_call_target="tpu_custom_call" | custom-call | flops 2000000000 | bytes 13762560 | tf_op jit(solution)/shard_map/prep/pallas_call | solution.py:152
  14.2 1.8 %copy-done = bf16[896,1536]{1,0:T(8,128)(2,1)S(1)} copy-done((bf16[896,1536]{1,0:T(8,128)(2,1)S(1)}, bf16[896,1536]{1,0:T(8,128)(2,1)}, u32[]{:S(2)}) %copy-start) | copy-done | bytes 2752536
  15.9 0.7 copy-done.4
  16.6 2.1 %qkv.2 = (f32[128,1024]{1,0:T(8,128)S(1)}, f32[128,1024]{1,0:T(8,128)S(1)}) custom-call(s32[2]{0:T(128)S(1)} %copy-done.4, s32[4]{0:T(128)S(1)} %copy-done.5, f32[4]{0:T(128)S(1)} %copy-done.6, bf16[136,896]{1,0:T(8,128)(2,1)S(1)} %get-tuple-element.28.refs_0_.refs_3_, bf16[136,896]{1,0:T(8,128)(2,1)S(1)} %collective-permute-done.refs_1_.refs_4_, ...), custom_call_target="tpu_custom_call" | custom-call | flops 939524096 | bytes 2752512 | tf_op jit(solution)/shard_map/qkv/pallas_call | solution.py:203
  18.7 2.1 %qkv.3 = (f32[128,1024]{1,0:T(8,128)S(1)}, f32[128,1024]{1,0:T(8,128)S(1)}) custom-call(s32[2]{0:T(128)S(1)} %copy-done.4, s32[4]{0:T(128)S(1)} %copy-done.5, f32[4]{0:T(128)S(1)} %copy-done.6, bf16[136,896]{1,0:T(8,128)(2,1)S(1)} %collective-permute-done.2.refs_0_.refs_5_, bf16[136,896]{1,0:T(8,128)(2,1)S(1)} %collective-permute-done.3.refs_1_.refs_6_, ...), custom_call_target="tpu_custom_call" | custom-call | flops 939524096 | bytes 2752512 | tf_op jit(solution)/shard_map/qkv/pallas_call | solution.py:203
  21.0 0.4 collective-permute-start.1
  21.4 1.4 collective-permute-done.4.other
  22.8 1.8 %collective-permute-start.5 = (bf16[128,1024]{1,0:T(8,128)(2,1)S(1)}, bf16[128,1024]{1,0:T(8,128)(2,1)S(1)}, u32[]{:S(2)}, u32[]{:S(2)}) collective-permute-start(bf16[128,1024]{1,0:T(8,128)(2,1)S(1)} %join.3), channel_id=1, source_target_pairs={{0,16},{8,24},{16,0},{24,8},{1,17},{9,25},{17,1},{25,9},{2,18},{10... | collective-permute-start | bytes 786440 | tf_op jit(solution)/shard_map/ppermute | solution.py:40
  24.6 0.3 multiply_sine_fusion
  25.0 6.4 %collective-permute-done.5.refs_3_ = bf16[128,1024]{1,0:T(8,128)(2,1)S(1)} collective-permute-done((bf16[128,1024]{1,0:T(8,128)(2,1)S(1)}, bf16[128,1024]{1,0:T(8,128)(2,1)S(1)}, u32[]{:S(2)}, u32[]{:S(2)}) %collective-permute-start.5) | collective-permute-done | bytes 262176 | tf_op jit(solution)/shard_map/ppermute | solution.py:40
  31.5 0.7 attend.1.refs_0_
  32.1 1.8 %collective-permute-start.7 = (bf16[128,512]{1,0:T(8,128)(2,1)S(1)}, bf16[128,512]{1,0:T(8,128)(2,1)S(1)}, u32[]{:S(2)}, u32[]{:S(2)}) collective-permute-start(bf16[128,512]{1,0:T(8,128)(2,1)S(1)} %attend.1.refs_0_), channel_id=1, source_target_pairs={{0,16},{8,24},{16,0},{24,8},{1,17},{9,25},{17,1},{25,9},{2,18},{10... | collective-permute-start | bytes 393224 | tf_op jit(solution)/shard_map/ppermute | solution.py:40
  34.1 3.1 %collective-permute-done.7.refs_2_ = bf16[128,512]{1,0:T(8,128)(2,1)S(1)} collective-permute-done((bf16[128,512]{1,0:T(8,128)(2,1)S(1)}, bf16[128,512]{1,0:T(8,128)(2,1)S(1)}, u32[]{:S(2)}, u32[]{:S(2)}) %collective-permute-start.7) | collective-permute-done | bytes 131104 | tf_op jit(solution)/shard_map/ppermute | solution.py:40
  37.3 1.2 collective-permute-done.8.refs_3_
  38.5 3.3 %project.1 = (f32[2,128,896]{2,1,0:T(8,128)S(1)}, bf16[2,128,896]{2,1,0:T(8,128)(2,1)S(1)}) custom-call(s32[2]{0:T(128)S(1)} %pad_add_fusion.2.ids, s32[4]{0:T(128)S(1)} %copy-done.5, f32[4]{0:T(128)S(1)} %copy-done.6, bf16[128,512]{1,0:T(8,128)(2,1)S(1)} %attend.1.refs_0_, bf16[128,512]{1,0:T(8,128)(2,1)S(1)} %collective-permute-done.6.refs_1_, ...), custom_call_target="tpu_custom_call" | custom-call | flops 939524096 | bytes 1835008 | tf_op jit(solution)/shard_map/project/pallas_call | solution.py:321
  41.9 1.8 %collective-permute-start.9 = (bf16[1,128,896]{2,1,0:T(8,128)(2,1)S(1)}, bf16[1,128,896]{2,1,0:T(8,128)(2,1)S(1)}, u32[]{:S(2)}, u32[]{:S(2)}) collective-permute-start(bf16[1,128,896]{2,1,0:T(8,128)(2,1)S(1)} %get-tuple-element.63), channel_id=1, source_target_pairs={{0,1},{1,0},{2,3},{3,2},{4,5},{5,4},{6,7},{7,6},{8,9},{9,8},{10,11... | collective-permute-start | bytes 688136 | tf_op jit(solution)/shard_map/ppermute | solution.py:40
  43.7 0.3 collective-permute-start.26
  44.0 6.4 %collective-permute-done.9 = bf16[1,128,896]{2,1,0:T(8,128)(2,1)S(1)} collective-permute-done((bf16[1,128,896]{2,1,0:T(8,128)(2,1)S(1)}, bf16[1,128,896]{2,1,0:T(8,128)(2,1)S(1)}, u32[]{:S(2)}, u32[]{:S(2)}) %collective-permute-start.9) | collective-permute-done | bytes 229408 | tf_op jit(solution)/shard_map/ppermute | solution.py:40
  50.4 0.6 spread.2
  51.0 1.9 %collective-permute-start.10 = (bf16[32,896]{1,0:T(8,128)(2,1)S(1)}, bf16[32,896]{1,0:T(8,128)(2,1)S(1)}, u32[]{:S(2)}, u32[]{:S(2)}) collective-permute-start(bf16[32,896]{1,0:T(8,128)(2,1)S(1)} %get-tuple-element.41), channel_id=1, source_target_pairs={{0,2},{1,3},{2,0},{3,1},{4,6},{5,7},{6,4},{7,5},{8,10},{9,11},{10,... | collective-permute-start | bytes 172040 | tf_op jit(solution)/shard_map/ppermute | solution.py:40
  52.9 2.6 %collective-permute-start.11 = (bf16[32,896]{1,0:T(8,128)(2,1)S(1)}, bf16[32,896]{1,0:T(8,128)(2,1)S(1)}, u32[]{:S(2)}, u32[]{:S(2)}) collective-permute-start(bf16[32,896]{1,0:T(8,128)(2,1)S(1)} %get-tuple-element.42), channel_id=1, source_target_pairs={{0,4},{1,5},{2,6},{3,7},{4,0},{5,1},{6,2},{7,3},{8,12},{9,13},{10,... | collective-permute-start | bytes 172040 | tf_op jit(solution)/shard_map/ppermute | solution.py:40
  55.5 0.6 spread.3
  56.1 1.0 collective-permute-start.27
  57.1 3.5 %collective-permute-start.28 = (bf16[32,896]{1,0:T(8,128)(2,1)S(1)}, bf16[32,896]{1,0:T(8,128)(2,1)S(1)}, u32[]{:S(2)}, u32[]{:S(2)}) collective-permute-start(bf16[32,896]{1,0:T(8,128)(2,1)S(1)} %get-tuple-element.49), channel_id=1, source_target_pairs={{0,4},{1,5},{2,6},{3,7},{4,0},{5,1},{6,2},{7,3},{8,12},{9,13},{10,... | collective-permute-start | bytes 172040 | tf_op jit(solution)/shard_map/ppermute | solution.py:40
  60.6 0.9 collective-permute-done.12.refs_2_
  61.5 0.7 sums.2
  62.3 1.6 %collective-permute-start.14 = (f32[32,128]{1,0:T(8,128)S(1)}, f32[32,128]{1,0:T(8,128)S(1)}, u32[]{:S(2)}, u32[]{:S(2)}) collective-permute-start(f32[32,128]{1,0:T(8,128)S(1)} %get-tuple-element.46.refs_0_), channel_id=1, source_target_pairs={{0,16},{8,24},{16,0},{24,8},{1,17},{9,25},{17,1},{25,9},{2,18},{10... | collective-permute-start | bytes 49160 | tf_op jit(solution)/shard_map/ppermute | solution.py:40
  63.8 0.3 collective-permute-start.15
  64.1 2.4 %collective-permute-done.29.refs_2_ = bf16[32,896]{1,0:T(8,128)(2,1)S(1)} collective-permute-done((bf16[32,896]{1,0:T(8,128)(2,1)S(1)}, bf16[32,896]{1,0:T(8,128)(2,1)S(1)}, u32[]{:S(2)}, u32[]{:S(2)}) %collective-permute-start.29) | collective-permute-done | bytes 57376 | tf_op jit(solution)/shard_map/ppermute | solution.py:40
  66.5 0.9 sums.3
  67.5 1.6 %collective-permute-start.31 = (f32[32,128]{1,0:T(8,128)S(1)}, f32[32,128]{1,0:T(8,128)S(1)}, u32[]{:S(2)}, u32[]{:S(2)}) collective-permute-start(f32[32,128]{1,0:T(8,128)S(1)} %get-tuple-element.53.refs_0_), channel_id=1, source_target_pairs={{0,16},{8,24},{16,0},{24,8},{1,17},{9,25},{17,1},{25,9},{2,18},{10... | collective-permute-start | bytes 49160 | tf_op jit(solution)/shard_map/ppermute | solution.py:40
  69.1 0.3 collective-permute-start.32
  69.4 0.2 finish.2
  69.7 1.3 collective-permute-start.17
  71.0 3.1 %collective-permute-start.18 = (bf16[32,896]{1,0:T(8,128)(2,1)S(1)}, bf16[32,896]{1,0:T(8,128)(2,1)S(1)}, u32[]{:S(2)}, u32[]{:S(2)}) collective-permute-start(bf16[32,896]{1,0:T(8,128)(2,1)S(1)} %finish.2), channel_id=1, source_target_pairs={{0,6},{1,7},{2,4},{3,5},{4,2},{5,3},{6,0},{7,1},{8,14},{9,15},{10,... | collective-permute-start | bytes 172040 | tf_op jit(solution)/shard_map/ppermute | solution.py:40
  74.1 0.2 finish.3
  74.4 1.3 collective-permute-start.34
  75.7 3.1 %collective-permute-start.35 = (bf16[32,896]{1,0:T(8,128)(2,1)S(1)}, bf16[32,896]{1,0:T(8,128)(2,1)S(1)}, u32[]{:S(2)}, u32[]{:S(2)}) collective-permute-start(bf16[32,896]{1,0:T(8,128)(2,1)S(1)} %finish.3), channel_id=1, source_target_pairs={{0,6},{1,7},{2,4},{3,5},{4,2},{5,3},{6,0},{7,1},{8,14},{9,15},{10,... | collective-permute-start | bytes 172040 | tf_op jit(solution)/shard_map/ppermute | solution.py:40
  78.8 1.6 %collective-permute-start.20 = (bf16[128,896]{1,0:T(8,128)(2,1)S(1)}, bf16[128,896]{1,0:T(8,128)(2,1)S(1)}, u32[]{:S(2)}, u32[]{:S(2)}) collective-permute-start(bf16[128,896]{1,0:T(8,128)(2,1)S(1)} %pad_maximum_fusion.refs_0_), channel_id=1, source_target_pairs={{0,1},{1,0},{2,3},{3,2},{4,5},{5,4},{6,7},{7,6},{8,9},{9,8},{10,11... | collective-permute-start | bytes 688136 | tf_op jit(solution)/shard_map/ppermute | solution.py:50
  80.4 1.5 %collective-permute-start.22 = (bf16[128,896]{1,0:T(8,128)(2,1)S(1)}, bf16[128,896]{1,0:T(8,128)(2,1)S(1)}, u32[]{:S(2)}, u32[]{:S(2)}) collective-permute-start(bf16[128,896]{1,0:T(8,128)(2,1)S(1)} %pad_maximum_fusion.refs_0_), channel_id=1, source_target_pairs={{0,16},{1,17},{2,18},{3,19},{4,20},{5,21},{6,22},{7,23},{8,24},{9,... | collective-permute-start | bytes 688136 | tf_op jit(solution)/shard_map/ppermute | solution.py:50
  81.9 0.4 collective-permute-start.24
  82.4 0.5 collective-permute-done.34
  82.9 1.6 %collective-permute-start.37 = (bf16[128,896]{1,0:T(8,128)(2,1)S(1)}, bf16[128,896]{1,0:T(8,128)(2,1)S(1)}, u32[]{:S(2)}, u32[]{:S(2)}) collective-permute-start(bf16[128,896]{1,0:T(8,128)(2,1)S(1)} %pad_maximum_fusion.1.refs_0_), channel_id=1, source_target_pairs={{0,1},{1,0},{2,3},{3,2},{4,5},{5,4},{6,7},{7,6},{8,9},{9,8},{10,11... | collective-permute-start | bytes 688136 | tf_op jit(solution)/shard_map/ppermute | solution.py:50
  84.5 2.9 %collective-permute-done.20.refs_2_ = bf16[128,896]{1,0:T(8,128)(2,1)S(1)} collective-permute-done((bf16[128,896]{1,0:T(8,128)(2,1)S(1)}, bf16[128,896]{1,0:T(8,128)(2,1)S(1)}, u32[]{:S(2)}, u32[]{:S(2)}) %collective-permute-start.20) | collective-permute-done | bytes 229408 | tf_op jit(solution)/shard_map/ppermute | solution.py:50
  87.4 1.5 %collective-permute-start.39 = (bf16[128,896]{1,0:T(8,128)(2,1)S(1)}, bf16[128,896]{1,0:T(8,128)(2,1)S(1)}, u32[]{:S(2)}, u32[]{:S(2)}) collective-permute-start(bf16[128,896]{1,0:T(8,128)(2,1)S(1)} %pad_maximum_fusion.1.refs_0_), channel_id=1, source_target_pairs={{0,16},{1,17},{2,18},{3,19},{4,20},{5,21},{6,22},{7,23},{8,24},{9,... | collective-permute-start | bytes 688136 | tf_op jit(solution)/shard_map/ppermute | solution.py:50
  88.9 2.4 %collective-permute-done.22.refs_4_ = bf16[128,896]{1,0:T(8,128)(2,1)S(1)} collective-permute-done((bf16[128,896]{1,0:T(8,128)(2,1)S(1)}, bf16[128,896]{1,0:T(8,128)(2,1)S(1)}, u32[]{:S(2)}, u32[]{:S(2)}) %collective-permute-start.22) | collective-permute-done | bytes 229408 | tf_op jit(solution)/shard_map/ppermute | solution.py:50
  91.3 0.9 collective-permute-start.41
  92.2 1.0 collective-permute-done.24.refs_6_
  93.2 0.5 collective-permute-start.23
  93.7 3.4 %collective-permute-done.37.refs_2_ = bf16[128,896]{1,0:T(8,128)(2,1)S(1)} collective-permute-done((bf16[128,896]{1,0:T(8,128)(2,1)S(1)}, bf16[128,896]{1,0:T(8,128)(2,1)S(1)}, u32[]{:S(2)}, u32[]{:S(2)}) %collective-permute-start.37) | collective-permute-done | bytes 229408 | tf_op jit(solution)/shard_map/ppermute | solution.py:50
  97.7 3.3 %collective-permute-done.39.refs_4_ = bf16[128,896]{1,0:T(8,128)(2,1)S(1)} collective-permute-done((bf16[128,896]{1,0:T(8,128)(2,1)S(1)}, bf16[128,896]{1,0:T(8,128)(2,1)S(1)}, u32[]{:S(2)}, u32[]{:S(2)}) %collective-permute-start.39) | collective-permute-done | bytes 229408 | tf_op jit(solution)/shard_map/ppermute | solution.py:50
  101.1 0.5 collective-permute-start.38
  101.6 0.4 collective-permute-start.42
  102.1 14.9 %vocab.2 = f32[8,256]{1,0:T(8,128)S(1)} custom-call(s32[40]{0:T(128)S(1)} %concatenate.16.at, s32[256,1]{1,0:T(8,128)S(1)} %copy.23.targets, bf16[128,896]{1,0:T(8,128)(2,1)S(1)} %pad_maximum_fusion.refs_0_, bf16[128,896]{1,0:T(8,128)(2,1)S(1)} %collective-permute-done.19.refs_1_, bf16[128,896]{1,0:T(8,128)(2,1)S(1)} %collective-permute-done.20.refs_2_, ...), custom_call_target="tpu_custom_call" | custom-call | flops 7516192768 | bytes 29360128 | tf_op jit(solution)/shard_map/vocab/pallas_call | solution.py:499
  117.0 14.9 %vocab.3 = f32[8,256]{1,0:T(8,128)S(1)} custom-call(s32[40]{0:T(128)S(1)} %concatenate.16.at, s32[256,1]{1,0:T(8,128)S(1)} %copy.24.targets, bf16[128,896]{1,0:T(8,128)(2,1)S(1)} %pad_maximum_fusion.1.refs_0_, bf16[128,896]{1,0:T(8,128)(2,1)S(1)} %collective-permute-done.36.refs_1_, bf16[128,896]{1,0:T(8,128)(2,1)S(1)} %collective-permute-done.37.refs_2_, ...), custom_call_target="tpu_custom_call" | custom-call | flops 7516192768 | bytes 29360128 | tf_op jit(solution)/shard_map/vocab/pallas_call | solution.py:499
  131.9 0.7 broadcast_in_dim.63
  132.7 2.7 %all-to-all-start = ((f32[32,3,512]{2,1,0:T(4,128)}), f32[32,3,512]{2,1,0:T(4,128)S(1)}, u32[]{:S(2)}, u32[]{:S(2)}) async-start(f32[32,3,512]{2,1,0:T(4,128)} %broadcast_in_dim.63), calls=%async_computation | async-start | bytes 524288 | tf_op jit(solution)/shard_map/all_to_all | solution.py:662
  135.4 10.4 %all-to-all-done = f32[32,3,512]{2,1,0:T(4,128)S(1)} async-done(((f32[32,3,512]{2,1,0:T(4,128)}), f32[32,3,512]{2,1,0:T(4,128)S(1)}, u32[]{:S(2)}, u32[]{:S(2)}) %all-to-all-start) | async-done | bytes 196640 | tf_op jit(solution)/shard_map/all_to_all | solution.py:662
  145.9 0.5 fusion.4
  146.7 0.5 maximum_divide_fusion
  (105 shorter events, 2.4 us)
Async XLA Ops:
  0.6 5.3 %copy-start.10 = (f32[3584]{0:T(1024)S(1)}, f32[3584]{0:T(1024)}, u32[]{:S(2)}) copy-start(f32[3584]{0:T(1024)} %param.30) | copy-start | bytes 43012
  0.7 1.2 copy-start.7
  1.9 4.2 %copy-start.3 = (s32[2]{0:T(128)}, s32[2]{0:T(128)S(1)}, u32[]{:S(2)}) copy-start(s32[2]{0:T(128)S(1)} %pad_add_fusion.3.ids) | copy-start | bytes 28
  1.9 4.0 %copy-start.11 = (f32[3584]{0:T(1024)S(1)}, f32[3584]{0:T(1024)}, u32[]{:S(2)}) copy-start(f32[3584]{0:T(1024)} %param.31) | copy-start | bytes 43012
  1.9 4.1 %copy-start.12 = (f32[3584]{0:T(1024)S(1)}, f32[3584]{0:T(1024)}, u32[]{:S(2)}) copy-start(f32[3584]{0:T(1024)} %param.32) | copy-start | bytes 43012
  2.8 11.4 %collective-permute-start = (bf16[136,896]{1,0:T(8,128)(2,1)S(1)}, bf16[136,896]{1,0:T(8,128)(2,1)S(1)}, u32[]{:S(2)}, u32[]{:S(2)}) collective-permute-start(bf16[136,896]{1,0:T(8,128)(2,1)S(1)} %get-tuple-element.29), channel_id=1, source_target_pairs={{0,8},{8,0},{16,24},{24,16},{1,9},{9,1},{17,25},{25,17},{2,10},{10... | collective-permute-start | bytes 731144 | tf_op jit(solution)/shard_map/ppermute | solution.py:40
  3.3 15.4 %collective-permute-start.2 = (bf16[136,896]{1,0:T(8,128)(2,1)S(1)}, bf16[136,896]{1,0:T(8,128)(2,1)S(1)}, u32[]{:S(2)}, u32[]{:S(2)}) collective-permute-start(bf16[136,896]{1,0:T(8,128)(2,1)S(1)} %get-tuple-element.33), channel_id=1, source_target_pairs={{0,16},{8,24},{16,0},{24,8},{1,17},{9,25},{17,1},{25,9},{2,18},{10... | collective-permute-start | bytes 731144 | tf_op jit(solution)/shard_map/ppermute | solution.py:40
  5.9 12.8 %collective-permute-start.3 = (bf16[136,896]{1,0:T(8,128)(2,1)S(1)}, bf16[136,896]{1,0:T(8,128)(2,1)S(1)}, u32[]{:S(2)}, u32[]{:S(2)}) collective-permute-start(bf16[136,896]{1,0:T(8,128)(2,1)S(1)} %get-tuple-element.34), channel_id=1, source_target_pairs={{0,24},{8,16},{16,8},{24,0},{1,25},{9,17},{17,9},{25,1},{2,26},{10... | collective-permute-start | bytes 731144 | tf_op jit(solution)/shard_map/ppermute | solution.py:40
  6.1 8.0 %copy-start.2 = (bf16[896,512]{1,0:T(8,128)(2,1)S(1)}, bf16[896,512]{1,0:T(8,128)(2,1)}, u32[]{:S(2)}) copy-start(bf16[896,512]{1,0:T(8,128)(2,1)} %refs_3_.5) | copy-start | bytes 2752516
  6.1 8.0 %copy-start.5 = (s32[4]{0:T(128)S(1)}, s32[4]{0:T(128)}, u32[]{:S(2)}) copy-start(s32[4]{0:T(128)} %cand_of.5) | copy-start | bytes 52
  6.2 8.0 %copy-start.6 = (f32[4]{0:T(128)S(1)}, f32[4]{0:T(128)}, u32[]{:S(2)}) copy-start(f32[4]{0:T(128)} %lambdas.5) | copy-start | bytes 52
  14.2 1.8 %copy-start = (bf16[896,1536]{1,0:T(8,128)(2,1)S(1)}, bf16[896,1536]{1,0:T(8,128)(2,1)}, u32[]{:S(2)}) copy-start(bf16[896,1536]{1,0:T(8,128)(2,1)} %get-tuple-element.30.refs_4_) | copy-start | bytes 8257540
  15.9 0.7 copy-start.4
  16.6 2.1 %copy-start.1 = (bf16[896,1536]{1,0:T(8,128)(2,1)S(1)}, bf16[896,1536]{1,0:T(8,128)(2,1)}, u32[]{:S(2)}) copy-start(bf16[896,1536]{1,0:T(8,128)(2,1)} %get-tuple-element.30.refs_4_) | copy-start | bytes 8257540
  20.8 2.0 %collective-permute-start.4 = (f32[128,1024]{1,0:T(8,128)S(1)}, f32[128,1024]{1,0:T(8,128)S(1)}, u32[]{:S(2)}, u32[]{:S(2)}) collective-permute-start(f32[128,1024]{1,0:T(8,128)S(1)} %get-tuple-element.36), channel_id=1, source_target_pairs={{0,8},{8,0},{16,24},{24,16},{1,9},{9,1},{17,25},{25,17},{2,10},{10... | collective-permute-start | bytes 1572872 | tf_op jit(solution)/shard_map/ppermute | solution.py:40
  21.0 3.9 %collective-permute-start.1 = (f32[128,1024]{1,0:T(8,128)S(1)}, f32[128,1024]{1,0:T(8,128)S(1)}, u32[]{:S(2)}, u32[]{:S(2)}) collective-permute-start(f32[128,1024]{1,0:T(8,128)S(1)} %get-tuple-element.32.refs_5_), channel_id=1, source_target_pairs={{0,8},{8,0},{16,24},{24,16},{1,9},{9,1},{17,25},{25,17},{2,10},{10... | collective-permute-start | bytes 1572872 | tf_op jit(solution)/shard_map/ppermute | solution.py:40
  22.8 8.6 %collective-permute-start.5 = (bf16[128,1024]{1,0:T(8,128)(2,1)S(1)}, bf16[128,1024]{1,0:T(8,128)(2,1)S(1)}, u32[]{:S(2)}, u32[]{:S(2)}) collective-permute-start(bf16[128,1024]{1,0:T(8,128)(2,1)S(1)} %join.3), channel_id=1, source_target_pairs={{0,16},{8,24},{16,0},{24,8},{1,17},{9,25},{17,1},{25,9},{2,18},{10... | collective-permute-start | bytes 786440 | tf_op jit(solution)/shard_map/ppermute | solution.py:40
  25.0 13.5 %copy-start.8 = (bf16[512,896]{1,0:T(8,128)(2,1)S(1)}, bf16[512,896]{1,0:T(8,128)(2,1)}, u32[]{:S(2)}) copy-start(bf16[512,896]{1,0:T(8,128)(2,1)} %refs_4_.3) | copy-start | bytes 2752516
  31.5 7.0 %copy-start.9 = (bf16[512,896]{1,0:T(8,128)(2,1)S(1)}, bf16[512,896]{1,0:T(8,128)(2,1)}, u32[]{:S(2)}) copy-start(bf16[512,896]{1,0:T(8,128)(2,1)} %get-tuple-element.37.refs_5_) | copy-start | bytes 2752516
  32.1 5.0 %collective-permute-start.7 = (bf16[128,512]{1,0:T(8,128)(2,1)S(1)}, bf16[128,512]{1,0:T(8,128)(2,1)S(1)}, u32[]{:S(2)}, u32[]{:S(2)}) collective-permute-start(bf16[128,512]{1,0:T(8,128)(2,1)S(1)} %attend.1.refs_0_), channel_id=1, source_target_pairs={{0,16},{8,24},{16,0},{24,8},{1,17},{9,25},{17,1},{25,9},{2,18},{10... | collective-permute-start | bytes 393224 | tf_op jit(solution)/shard_map/ppermute | solution.py:40
  34.1 3.2 %collective-permute-start.6 = (bf16[128,512]{1,0:T(8,128)(2,1)S(1)}, bf16[128,512]{1,0:T(8,128)(2,1)S(1)}, u32[]{:S(2)}, u32[]{:S(2)}) collective-permute-start(bf16[128,512]{1,0:T(8,128)(2,1)S(1)} %attend.1.refs_0_), channel_id=1, source_target_pairs={{0,8},{8,0},{16,24},{24,16},{1,9},{9,1},{17,25},{25,17},{2,10},{10... | collective-permute-start | bytes 393224 | tf_op jit(solution)/shard_map/ppermute | solution.py:40
  37.2 1.3 collective-permute-start.8
  41.9 8.5 %collective-permute-start.9 = (bf16[1,128,896]{2,1,0:T(8,128)(2,1)S(1)}, bf16[1,128,896]{2,1,0:T(8,128)(2,1)S(1)}, u32[]{:S(2)}, u32[]{:S(2)}) collective-permute-start(bf16[1,128,896]{2,1,0:T(8,128)(2,1)S(1)} %get-tuple-element.63), channel_id=1, source_target_pairs={{0,1},{1,0},{2,3},{3,2},{4,5},{5,4},{6,7},{7,6},{8,9},{9,8},{10,11... | collective-permute-start | bytes 688136 | tf_op jit(solution)/shard_map/ppermute | solution.py:40
  43.7 11.8 %collective-permute-start.26 = (bf16[1,128,896]{2,1,0:T(8,128)(2,1)S(1)}, bf16[1,128,896]{2,1,0:T(8,128)(2,1)S(1)}, u32[]{:S(2)}, u32[]{:S(2)}) collective-permute-start(bf16[1,128,896]{2,1,0:T(8,128)(2,1)S(1)} %get-tuple-element.64), channel_id=1, source_target_pairs={{0,1},{1,0},{2,3},{3,2},{4,5},{5,4},{6,7},{7,6},{8,9},{9,8},{10,11... | collective-permute-start | bytes 688136 | tf_op jit(solution)/shard_map/ppermute | solution.py:40
  51.0 9.5 %collective-permute-start.10 = (bf16[32,896]{1,0:T(8,128)(2,1)S(1)}, bf16[32,896]{1,0:T(8,128)(2,1)S(1)}, u32[]{:S(2)}, u32[]{:S(2)}) collective-permute-start(bf16[32,896]{1,0:T(8,128)(2,1)S(1)} %get-tuple-element.41), channel_id=1, source_target_pairs={{0,2},{1,3},{2,0},{3,1},{4,6},{5,7},{6,4},{7,5},{8,10},{9,11},{10,... | collective-permute-start | bytes 172040 | tf_op jit(solution)/shard_map/ppermute | solution.py:40
  52.9 7.7 %collective-permute-start.11 = (bf16[32,896]{1,0:T(8,128)(2,1)S(1)}, bf16[32,896]{1,0:T(8,128)(2,1)S(1)}, u32[]{:S(2)}, u32[]{:S(2)}) collective-permute-start(bf16[32,896]{1,0:T(8,128)(2,1)S(1)} %get-tuple-element.42), channel_id=1, source_target_pairs={{0,4},{1,5},{2,6},{3,7},{4,0},{5,1},{6,2},{7,3},{8,12},{9,13},{10,... | collective-permute-start | bytes 172040 | tf_op jit(solution)/shard_map/ppermute | solution.py:40
  55.5 6.0 %collective-permute-start.12 = (bf16[32,896]{1,0:T(8,128)(2,1)S(1)}, bf16[32,896]{1,0:T(8,128)(2,1)S(1)}, u32[]{:S(2)}, u32[]{:S(2)}) collective-permute-start(bf16[32,896]{1,0:T(8,128)(2,1)S(1)} %get-tuple-element.43), channel_id=1, source_target_pairs={{0,6},{1,7},{2,4},{3,5},{4,2},{5,3},{6,0},{7,1},{8,14},{9,15},{10,... | collective-permute-start | bytes 172040 | tf_op jit(solution)/shard_map/ppermute | solution.py:40
  56.1 7.8 %collective-permute-start.27 = (bf16[32,896]{1,0:T(8,128)(2,1)S(1)}, bf16[32,896]{1,0:T(8,128)(2,1)S(1)}, u32[]{:S(2)}, u32[]{:S(2)}) collective-permute-start(bf16[32,896]{1,0:T(8,128)(2,1)S(1)} %get-tuple-element.48), channel_id=1, source_target_pairs={{0,2},{1,3},{2,0},{3,1},{4,6},{5,7},{6,4},{7,5},{8,10},{9,11},{10,... | collective-permute-start | bytes 172040 | tf_op jit(solution)/shard_map/ppermute | solution.py:40
  57.1 7.1 %collective-permute-start.28 = (bf16[32,896]{1,0:T(8,128)(2,1)S(1)}, bf16[32,896]{1,0:T(8,128)(2,1)S(1)}, u32[]{:S(2)}, u32[]{:S(2)}) collective-permute-start(bf16[32,896]{1,0:T(8,128)(2,1)S(1)} %get-tuple-element.49), channel_id=1, source_target_pairs={{0,4},{1,5},{2,6},{3,7},{4,0},{5,1},{6,2},{7,3},{8,12},{9,13},{10,... | collective-permute-start | bytes 172040 | tf_op jit(solution)/shard_map/ppermute | solution.py:40
  60.5 6.0 %collective-permute-start.29 = (bf16[32,896]{1,0:T(8,128)(2,1)S(1)}, bf16[32,896]{1,0:T(8,128)(2,1)S(1)}, u32[]{:S(2)}, u32[]{:S(2)}) collective-permute-start(bf16[32,896]{1,0:T(8,128)(2,1)S(1)} %get-tuple-element.50), channel_id=1, source_target_pairs={{0,6},{1,7},{2,4},{3,5},{4,2},{5,3},{6,0},{7,1},{8,14},{9,15},{10,... | collective-permute-start | bytes 172040 | tf_op jit(solution)/shard_map/ppermute | solution.py:40
  62.2 6.9 %collective-permute-start.13 = (f32[32,128]{1,0:T(8,128)S(1)}, f32[32,128]{1,0:T(8,128)S(1)}, u32[]{:S(2)}, u32[]{:S(2)}) collective-permute-start(f32[32,128]{1,0:T(8,128)S(1)} %get-tuple-element.46.refs_0_), channel_id=1, source_target_pairs={{0,8},{8,0},{16,24},{24,16},{1,9},{9,1},{17,25},{25,17},{2,10},{10... | collective-permute-start | bytes 49160 | tf_op jit(solution)/shard_map/ppermute | solution.py:40
  62.3 7.1 %collective-permute-start.14 = (f32[32,128]{1,0:T(8,128)S(1)}, f32[32,128]{1,0:T(8,128)S(1)}, u32[]{:S(2)}, u32[]{:S(2)}) collective-permute-start(f32[32,128]{1,0:T(8,128)S(1)} %get-tuple-element.46.refs_0_), channel_id=1, source_target_pairs={{0,16},{8,24},{16,0},{24,8},{1,17},{9,25},{17,1},{25,9},{2,18},{10... | collective-permute-start | bytes 49160 | tf_op jit(solution)/shard_map/ppermute | solution.py:40
  63.8 5.5 %collective-permute-start.15 = (f32[32,128]{1,0:T(8,128)S(1)}, f32[32,128]{1,0:T(8,128)S(1)}, u32[]{:S(2)}, u32[]{:S(2)}) collective-permute-start(f32[32,128]{1,0:T(8,128)S(1)} %get-tuple-element.46.refs_0_), channel_id=1, source_target_pairs={{0,24},{8,16},{16,8},{24,0},{1,25},{9,17},{17,9},{25,1},{2,26},{10... | collective-permute-start | bytes 49160 | tf_op jit(solution)/shard_map/ppermute | solution.py:40
  67.4 3.6 %collective-permute-start.30 = (f32[32,128]{1,0:T(8,128)S(1)}, f32[32,128]{1,0:T(8,128)S(1)}, u32[]{:S(2)}, u32[]{:S(2)}) collective-permute-start(f32[32,128]{1,0:T(8,128)S(1)} %get-tuple-element.53.refs_0_), channel_id=1, source_target_pairs={{0,8},{8,0},{16,24},{24,16},{1,9},{9,1},{17,25},{25,17},{2,10},{10... | collective-permute-start | bytes 49160 | tf_op jit(solution)/shard_map/ppermute | solution.py:40
  67.5 6.6 %collective-permute-start.31 = (f32[32,128]{1,0:T(8,128)S(1)}, f32[32,128]{1,0:T(8,128)S(1)}, u32[]{:S(2)}, u32[]{:S(2)}) collective-permute-start(f32[32,128]{1,0:T(8,128)S(1)} %get-tuple-element.53.refs_0_), channel_id=1, source_target_pairs={{0,16},{8,24},{16,0},{24,8},{1,17},{9,25},{17,1},{25,9},{2,18},{10... | collective-permute-start | bytes 49160 | tf_op jit(solution)/shard_map/ppermute | solution.py:40
  69.1 5.0 %collective-permute-start.32 = (f32[32,128]{1,0:T(8,128)S(1)}, f32[32,128]{1,0:T(8,128)S(1)}, u32[]{:S(2)}, u32[]{:S(2)}) collective-permute-start(f32[32,128]{1,0:T(8,128)S(1)} %get-tuple-element.53.refs_0_), channel_id=1, source_target_pairs={{0,24},{8,16},{16,8},{24,0},{1,25},{9,17},{17,9},{25,1},{2,26},{10... | collective-permute-start | bytes 49160 | tf_op jit(solution)/shard_map/ppermute | solution.py:40
  69.4 15.1 %copy-start.13 = (s32[512]{0:T(512)S(1)}, s32[512]{0:T(512)}, u32[]{:S(2)}) copy-start(s32[512]{0:T(512)} %param.18) | copy-start | bytes 6148
  69.4 28.1 %copy-start.14 = (s32[128]{0:T(128)S(1)}, s32[128]{0:T(128)}, u32[]{:S(2)}) copy-start(s32[128]{0:T(128)} %param.19) | copy-start | bytes 1540
  69.6 6.0 %collective-permute-start.16 = (bf16[32,896]{1,0:T(8,128)(2,1)S(1)}, bf16[32,896]{1,0:T(8,128)(2,1)S(1)}, u32[]{:S(2)}, u32[]{:S(2)}) collective-permute-start(bf16[32,896]{1,0:T(8,128)(2,1)S(1)} %finish.2), channel_id=1, source_target_pairs={{0,2},{1,3},{2,0},{3,1},{4,6},{5,7},{6,4},{7,5},{8,10},{9,11},{10,... | collective-permute-start | bytes 172040 | tf_op jit(solution)/shard_map/ppermute | solution.py:40
  69.7 9.1 %collective-permute-start.17 = (bf16[32,896]{1,0:T(8,128)(2,1)S(1)}, bf16[32,896]{1,0:T(8,128)(2,1)S(1)}, u32[]{:S(2)}, u32[]{:S(2)}) collective-permute-start(bf16[32,896]{1,0:T(8,128)(2,1)S(1)} %finish.2), channel_id=1, source_target_pairs={{0,4},{1,5},{2,6},{3,7},{4,0},{5,1},{6,2},{7,3},{8,12},{9,13},{10,... | collective-permute-start | bytes 172040 | tf_op jit(solution)/shard_map/ppermute | solution.py:40
  71.0 7.8 %collective-permute-start.18 = (bf16[32,896]{1,0:T(8,128)(2,1)S(1)}, bf16[32,896]{1,0:T(8,128)(2,1)S(1)}, u32[]{:S(2)}, u32[]{:S(2)}) collective-permute-start(bf16[32,896]{1,0:T(8,128)(2,1)S(1)} %finish.2), channel_id=1, source_target_pairs={{0,6},{1,7},{2,4},{3,5},{4,2},{5,3},{6,0},{7,1},{8,14},{9,15},{10,... | collective-permute-start | bytes 172040 | tf_op jit(solution)/shard_map/ppermute | solution.py:40
  74.3 7.6 %collective-permute-start.33 = (bf16[32,896]{1,0:T(8,128)(2,1)S(1)}, bf16[32,896]{1,0:T(8,128)(2,1)S(1)}, u32[]{:S(2)}, u32[]{:S(2)}) collective-permute-start(bf16[32,896]{1,0:T(8,128)(2,1)S(1)} %finish.3), channel_id=1, source_target_pairs={{0,2},{1,3},{2,0},{3,1},{4,6},{5,7},{6,4},{7,5},{8,10},{9,11},{10,... | collective-permute-start | bytes 172040 | tf_op jit(solution)/shard_map/ppermute | solution.py:40
  74.4 8.4 %collective-permute-start.34 = (bf16[32,896]{1,0:T(8,128)(2,1)S(1)}, bf16[32,896]{1,0:T(8,128)(2,1)S(1)}, u32[]{:S(2)}, u32[]{:S(2)}) collective-permute-start(bf16[32,896]{1,0:T(8,128)(2,1)S(1)} %finish.3), channel_id=1, source_target_pairs={{0,4},{1,5},{2,6},{3,7},{4,0},{5,1},{6,2},{7,3},{8,12},{9,13},{10,... | collective-permute-start | bytes 172040 | tf_op jit(solution)/shard_map/ppermute | solution.py:40
  75.7 7.2 %collective-permute-start.35 = (bf16[32,896]{1,0:T(8,128)(2,1)S(1)}, bf16[32,896]{1,0:T(8,128)(2,1)S(1)}, u32[]{:S(2)}, u32[]{:S(2)}) collective-permute-start(bf16[32,896]{1,0:T(8,128)(2,1)S(1)} %finish.3), channel_id=1, source_target_pairs={{0,6},{1,7},{2,4},{3,5},{4,2},{5,3},{6,0},{7,1},{8,14},{9,15},{10,... | collective-permute-start | bytes 172040 | tf_op jit(solution)/shard_map/ppermute | solution.py:40
  78.8 8.5 %collective-permute-start.20 = (bf16[128,896]{1,0:T(8,128)(2,1)S(1)}, bf16[128,896]{1,0:T(8,128)(2,1)S(1)}, u32[]{:S(2)}, u32[]{:S(2)}) collective-permute-start(bf16[128,896]{1,0:T(8,128)(2,1)S(1)} %pad_maximum_fusion.refs_0_), channel_id=1, source_target_pairs={{0,1},{1,0},{2,3},{3,2},{4,5},{5,4},{6,7},{7,6},{8,9},{9,8},{10,11... | collective-permute-start | bytes 688136 | tf_op jit(solution)/shard_map/ppermute | solution.py:50
  80.4 10.9 %collective-permute-start.22 = (bf16[128,896]{1,0:T(8,128)(2,1)S(1)}, bf16[128,896]{1,0:T(8,128)(2,1)S(1)}, u32[]{:S(2)}, u32[]{:S(2)}) collective-permute-start(bf16[128,896]{1,0:T(8,128)(2,1)S(1)} %pad_maximum_fusion.refs_0_), channel_id=1, source_target_pairs={{0,16},{1,17},{2,18},{3,19},{4,20},{5,21},{6,22},{7,23},{8,24},{9,... | collective-permute-start | bytes 688136 | tf_op jit(solution)/shard_map/ppermute | solution.py:50
  81.9 11.3 %collective-permute-start.24 = (bf16[128,896]{1,0:T(8,128)(2,1)S(1)}, bf16[128,896]{1,0:T(8,128)(2,1)S(1)}, u32[]{:S(2)}, u32[]{:S(2)}) collective-permute-start(bf16[128,896]{1,0:T(8,128)(2,1)S(1)} %pad_maximum_fusion.refs_0_), channel_id=1, source_target_pairs={{0,17},{1,16},{2,19},{3,18},{4,21},{5,20},{6,23},{7,22},{8,25},{9,... | collective-permute-start | bytes 688136 | tf_op jit(solution)/shard_map/ppermute | solution.py:50
  82.8 10.4 %collective-permute-start.19 = (bf16[128,896]{1,0:T(8,128)(2,1)S(1)}, bf16[128,896]{1,0:T(8,128)(2,1)S(1)}, u32[]{:S(2)}, u32[]{:S(2)}) collective-permute-start(bf16[128,896]{1,0:T(8,128)(2,1)S(1)} %pad_maximum_fusion.refs_0_), channel_id=1, source_target_pairs={{0,8},{8,0},{16,24},{24,16},{1,9},{9,1},{17,25},{25,17},{2,10},{10... | collective-permute-start | bytes 688136 | tf_op jit(solution)/shard_map/ppermute | solution.py:40
  82.9 14.3 %collective-permute-start.37 = (bf16[128,896]{1,0:T(8,128)(2,1)S(1)}, bf16[128,896]{1,0:T(8,128)(2,1)S(1)}, u32[]{:S(2)}, u32[]{:S(2)}) collective-permute-start(bf16[128,896]{1,0:T(8,128)(2,1)S(1)} %pad_maximum_fusion.1.refs_0_), channel_id=1, source_target_pairs={{0,1},{1,0},{2,3},{3,2},{4,5},{5,4},{6,7},{7,6},{8,9},{9,8},{10,11... | collective-permute-start | bytes 688136 | tf_op jit(solution)/shard_map/ppermute | solution.py:50
  87.4 13.7 %collective-permute-start.39 = (bf16[128,896]{1,0:T(8,128)(2,1)S(1)}, bf16[128,896]{1,0:T(8,128)(2,1)S(1)}, u32[]{:S(2)}, u32[]{:S(2)}) collective-permute-start(bf16[128,896]{1,0:T(8,128)(2,1)S(1)} %pad_maximum_fusion.1.refs_0_), channel_id=1, source_target_pairs={{0,16},{1,17},{2,18},{3,19},{4,20},{5,21},{6,22},{7,23},{8,24},{9,... | collective-permute-start | bytes 688136 | tf_op jit(solution)/shard_map/ppermute | solution.py:50
  91.3 9.8 %collective-permute-start.41 = (bf16[128,896]{1,0:T(8,128)(2,1)S(1)}, bf16[128,896]{1,0:T(8,128)(2,1)S(1)}, u32[]{:S(2)}, u32[]{:S(2)}) collective-permute-start(bf16[128,896]{1,0:T(8,128)(2,1)S(1)} %pad_maximum_fusion.1.refs_0_), channel_id=1, source_target_pairs={{0,17},{1,16},{2,19},{3,18},{4,21},{5,20},{6,23},{7,22},{8,25},{9,... | collective-permute-start | bytes 688136 | tf_op jit(solution)/shard_map/ppermute | solution.py:50
  93.2 8.4 %collective-permute-start.21 = (bf16[128,896]{1,0:T(8,128)(2,1)S(1)}, bf16[128,896]{1,0:T(8,128)(2,1)S(1)}, u32[]{:S(2)}, u32[]{:S(2)}) collective-permute-start(bf16[128,896]{1,0:T(8,128)(2,1)S(1)} %collective-permute-done.20.refs_2_), channel_id=1, source_target_pairs={{0,8},{8,0},{16,24},{24,16},{1,9},{9,1},{17,25},{25,17},{2,10},{10... | collective-permute-start | bytes 688136 | tf_op jit(solution)/shard_map/ppermute | solution.py:40
  93.2 8.4 %collective-permute-start.23 = (bf16[128,896]{1,0:T(8,128)(2,1)S(1)}, bf16[128,896]{1,0:T(8,128)(2,1)S(1)}, u32[]{:S(2)}, u32[]{:S(2)}) collective-permute-start(bf16[128,896]{1,0:T(8,128)(2,1)S(1)} %collective-permute-done.22.refs_4_), channel_id=1, source_target_pairs={{0,8},{8,0},{16,24},{24,16},{1,9},{9,1},{17,25},{25,17},{2,10},{10... | collective-permute-start | bytes 688136 | tf_op jit(solution)/shard_map/ppermute | solution.py:40
  97.2 4.9 %collective-permute-start.25 = (bf16[128,896]{1,0:T(8,128)(2,1)S(1)}, bf16[128,896]{1,0:T(8,128)(2,1)S(1)}, u32[]{:S(2)}, u32[]{:S(2)}) collective-permute-start(bf16[128,896]{1,0:T(8,128)(2,1)S(1)} %collective-permute-done.24.refs_6_), channel_id=1, source_target_pairs={{0,8},{8,0},{16,24},{24,16},{1,9},{9,1},{17,25},{25,17},{2,10},{10... | collective-permute-start | bytes 688136 | tf_op jit(solution)/shard_map/ppermute | solution.py:40
  101.1 15.9 %collective-permute-start.36 = (bf16[128,896]{1,0:T(8,128)(2,1)S(1)}, bf16[128,896]{1,0:T(8,128)(2,1)S(1)}, u32[]{:S(2)}, u32[]{:S(2)}) collective-permute-start(bf16[128,896]{1,0:T(8,128)(2,1)S(1)} %pad_maximum_fusion.1.refs_0_), channel_id=1, source_target_pairs={{0,8},{8,0},{16,24},{24,16},{1,9},{9,1},{17,25},{25,17},{2,10},{10... | collective-permute-start | bytes 688136 | tf_op jit(solution)/shard_map/ppermute | solution.py:40
  101.1 15.9 %collective-permute-start.38 = (bf16[128,896]{1,0:T(8,128)(2,1)S(1)}, bf16[128,896]{1,0:T(8,128)(2,1)S(1)}, u32[]{:S(2)}, u32[]{:S(2)}) collective-permute-start(bf16[128,896]{1,0:T(8,128)(2,1)S(1)} %collective-permute-done.37.refs_2_), channel_id=1, source_target_pairs={{0,8},{8,0},{16,24},{24,16},{1,9},{9,1},{17,25},{25,17},{2,10},{10... | collective-permute-start | bytes 688136 | tf_op jit(solution)/shard_map/ppermute | solution.py:40
  101.6 15.4 %collective-permute-start.40 = (bf16[128,896]{1,0:T(8,128)(2,1)S(1)}, bf16[128,896]{1,0:T(8,128)(2,1)S(1)}, u32[]{:S(2)}, u32[]{:S(2)}) collective-permute-start(bf16[128,896]{1,0:T(8,128)(2,1)S(1)} %collective-permute-done.39.refs_4_), channel_id=1, source_target_pairs={{0,8},{8,0},{16,24},{24,16},{1,9},{9,1},{17,25},{25,17},{2,10},{10... | collective-permute-start | bytes 688136 | tf_op jit(solution)/shard_map/ppermute | solution.py:40
  101.6 15.4 %collective-permute-start.42 = (bf16[128,896]{1,0:T(8,128)(2,1)S(1)}, bf16[128,896]{1,0:T(8,128)(2,1)S(1)}, u32[]{:S(2)}, u32[]{:S(2)}) collective-permute-start(bf16[128,896]{1,0:T(8,128)(2,1)S(1)} %collective-permute-done.41.refs_6_), channel_id=1, source_target_pairs={{0,8},{8,0},{16,24},{24,16},{1,9},{9,1},{17,25},{25,17},{2,10},{10... | collective-permute-start | bytes 688136 | tf_op jit(solution)/shard_map/ppermute | solution.py:40
  132.7 13.2 %all-to-all-start = ((f32[32,3,512]{2,1,0:T(4,128)}), f32[32,3,512]{2,1,0:T(4,128)S(1)}, u32[]{:S(2)}, u32[]{:S(2)}) async-start(f32[32,3,512]{2,1,0:T(4,128)} %broadcast_in_dim.63), calls=%async_computation | async-start | bytes 524288 | tf_op jit(solution)/shard_map/all_to_all | solution.py:662
